TPU v7x, 32 devices: a whole 2x2x4 slice. The times are simulated.
32 devices in a mesh: dp: 8 (over y, x, core), mp: 4 (over z).
Axes of the slice: x: 2, y: 2, z: 4, core: 2. Of those that a mesh axis runs over, the one named last changes fastest.
Arguments:
- inputs: bfloat16 [1568, 16, 1024], P('mp', 'dp'), may hold values from -6 to 6
- teacher: bfloat16 [1568, 16, 1024], P('mp', 'dp'), may hold values from -6 to 6
- clip_tokens: int32 [16], P('dp'), may hold values from 1 to 1568, 18816 in all
- owners: int32 [192], replicated, may hold values from 0 to 7, as said below
- qkv_master: float32 [8, 128, 3, 1024], P(None, 'dp', None, 'mp'), may hold values from -0.1875 to 0.1875
- out_master: float32 [8, 128, 1024], P('mp', 'dp'), may hold values from -3 to 3
- up_master: float32 [8, 128, 4096], P(None, 'dp', 'mp'), may hold values from -0.1875 to 0.1875
- down_master: float32 [32, 128, 1024], P('mp', 'dp'), may hold values from -0.09375 to 0.09375
- norm_gains: float32 [2, 1024], replicated, may hold values from 0.25 to 1.75
- shift_vectors: float32 [4, 1024], replicated, may hold values from -0.8 to 0.8
- split_vectors: float32 [4, 1536], P('mp'), may hold values from -1.2 to 1.2
- bases: float32 [384, 4, 2, 128, 128], P('dp', 'mp'), may hold values from -1 to 1, as said below
- first_moments: float32 [384, 4, 128, 128], P('dp', 'mp'), may hold values from -5 to 5
- second_moments: float32 [384, 4, 128, 128], P('dp', 'mp'), may hold values from 0.2 to 2
- plain_first: float32 [6, 1024], replicated, may hold values from -5 to 5
- plain_second: float32 [6, 1024], replicated, may hold values from 0.2 to 2
- split_first: float32 [4, 1536], P('mp'), may hold values from -5 to 5
- split_second: float32 [4, 1536], P('mp'), may hold values from 0.2 to 2
Outputs:
- output: bfloat16 [1568, 16, 1024], P('mp', 'dp')
- input_grad: float32 [1568, 16, 1024], P('mp', 'dp')
- qkv_new: float32 [8, 128, 3, 1024], P(None, 'dp', None, 'mp')
- out_new: float32 [8, 128, 1024], P('mp', 'dp')
- up_new: float32 [8, 128, 4096], P(None, 'dp', 'mp')
- down_new: float32 [32, 128, 1024], P('mp', 'dp')
- qkv_copy: bfloat16 [8, 128, 3, 1024], P(None, 'dp', None, 'mp')
- out_copy: bfloat16 [8, 128, 1024], P('mp', 'dp')
- up_copy: bfloat16 [8, 128, 4096], P(None, 'dp', 'mp')
- down_copy: bfloat16 [32, 128, 1024], P('mp', 'dp')
- gains_new: float32 [2, 1024], replicated
- shifts_new: float32 [4, 1024], replicated
- split_new: float32 [4, 1536], P('mp')
- first_new: float32 [384, 4, 128, 128], P('dp', 'mp')
- second_new: float32 [384, 4, 128, 128], P('dp', 'mp')
- plain_first_new: float32 [6, 1024], replicated
- plain_second_new: float32 [6, 1024], replicated
- split_first_new: float32 [4, 1536], P('mp')
- split_second_new: float32 [4, 1536], P('mp')
Inputs may be any that keep to these rules, and one draw needn't show every extreme that they name: `owners`: no dp index owns more than 48 blocks; one index owns exactly 48. bases[m, g, 0] and bases[m, g, 1] are orthogonal to float32 rounding.
All inputs are finite; a program needn't handle non-finite values. No bound on the sum of `clip_tokens` on one device may be relied on, other than what follows from the above.
Results may differ from a plain program's by a relative error of at most 0.013.
Values may be sent and summed in bfloat16 or wider, within the bound.
A program may use at most 384 MiB of HBM per device.

v0:
```python
from functools import partial

import jax
import jax.numpy as jnp
from jax import lax
from jax.sharding import PartitionSpec as P

HD = 64
B = 128


eps_norm = 1e-06
eps_adam = 1e-08
beta_first = 0.5
beta_second = 0.6
rate_qkv = 0.016
rate_out = 0.25
rate_up = 0.016
rate_down = 0.008
rate_vector = 0.3
scale_score = 0.125
highest = lax.Precision.HIGHEST


def layer_norm(values, scale_row, shift_row):
    average = jnp.mean(values, axis=-1, keepdims=True)
    centered = values - average
    variance = jnp.mean(centered * centered, axis=-1, keepdims=True)
    return centered * lax.rsqrt(variance + 1e-06) * scale_row + shift_row


def adam_rows(grad_rows, param_rows, first_rows, second_rows):
    scaled = grad_rows * lax.rsqrt(
        jnp.mean(grad_rows * grad_rows, axis=-1, keepdims=True) + eps_norm
    )
    new_first = beta_first * first_rows + (1.0 - beta_first) * scaled
    new_second = beta_second * second_rows + (1.0 - beta_second) * scaled * scaled
    step_rows = new_first / (jnp.sqrt(new_second) + eps_adam)
    return (param_rows - rate_vector * step_rows, new_first, new_second)


def rotate_adam(grad_blocks, left_basis, right_basis, old_first, old_second):
    scaled = grad_blocks * lax.rsqrt(
        jnp.mean(grad_blocks * grad_blocks, axis=(1, 2), keepdims=True) + eps_norm
    )
    rotated = jnp.einsum("kba,kbd->kad", left_basis, scaled, precision=highest)
    rotated = jnp.einsum("kad,kde->kae", rotated, right_basis, precision=highest)
    new_first = beta_first * old_first + (1.0 - beta_first) * rotated
    new_second = beta_second * old_second + (1.0 - beta_second) * rotated * rotated
    step_rot = new_first / (jnp.sqrt(new_second) + eps_adam)
    update = jnp.einsum("kab,kbd->kad", left_basis, step_rot, precision=highest)
    update = jnp.einsum("kad,ked->kae", update, right_basis, precision=highest)
    return (new_first, new_second, update)


def collect_rows(values):
    return lax.all_gather(values, "mp", axis=0, tiled=True)


def reduce_rows(term_fn, row_total):
    return lax.psum_scatter(
        term_fn(jnp.int32(0), lax.axis_size("mp") * row_total).astype(jnp.bfloat16),
        "mp",
        scatter_dimension=0,
        tiled=True,
    ).astype(jnp.float32)


def masked_scores(block_query, key_rows, key_valid):
    scores = (
        jnp.einsum("qche,kche->chqk", block_query, key_rows, preferred_element_type=jnp.float32)
        * scale_score
    )
    return jnp.where(key_valid[:, None, None, :], scores, -1e30)


def attend_forward(proj_rows, key_valid, block_rows):
    seq_len, clips_here, _, head_count, head_dim = proj_rows.shape
    queries = proj_rows[:, :, 0]
    key_rows = proj_rows[:, :, 1]
    value_rows = proj_rows[:, :, 2]
    outputs = []
    log_parts = []
    for first_row in range(0, seq_len, block_rows):
        scores = masked_scores(queries[first_row : first_row + block_rows], key_rows, key_valid)
        row_top = jnp.max(scores, axis=-1, keepdims=True)
        exponent = jnp.exp(scores - row_top)
        row_total = jnp.sum(exponent, axis=-1, keepdims=True)
        probability = (exponent / row_total).astype(jnp.bfloat16)
        log_parts.append(row_top[..., 0] + jnp.log(row_total[..., 0]))
        block_out = jnp.einsum(
            "chqk,kche->qche", probability, value_rows, preferred_element_type=jnp.float32
        )
        outputs.append(block_out.astype(jnp.bfloat16))
    attended = jnp.concatenate(outputs, axis=0).reshape(seq_len, clips_here, head_count * head_dim)
    return (attended, jnp.concatenate(log_parts, axis=2))


def attend_backward(proj_rows, log_sums, grad_attended, key_valid, block_rows):
    seq_len, clips_here, _, head_count, head_dim = proj_rows.shape
    queries = proj_rows[:, :, 0]
    key_rows = proj_rows[:, :, 1]
    value_rows = proj_rows[:, :, 2]
    grad_out = grad_attended.reshape(seq_len, clips_here, head_count, head_dim)
    grad_keys = jnp.zeros((seq_len, clips_here, head_count, head_dim), jnp.float32)
    grad_values = jnp.zeros((seq_len, clips_here, head_count, head_dim), jnp.float32)
    query_parts = []
    for first_row in range(0, seq_len, block_rows):
        block_query = queries[first_row : first_row + block_rows]
        block_grad = grad_out[first_row : first_row + block_rows]
        scores = masked_scores(block_query, key_rows, key_valid)
        probability = jnp.exp(scores - log_sums[:, :, first_row : first_row + block_rows, None])
        grad_values = grad_values + jnp.einsum(
            "chqk,qche->kche",
            probability.astype(jnp.bfloat16),
            block_grad,
            preferred_element_type=jnp.float32,
        )
        grad_probs = jnp.einsum(
            "qche,kche->chqk", block_grad, value_rows, preferred_element_type=jnp.float32
        )
        delta = jnp.sum(probability * grad_probs, axis=-1, keepdims=True)
        grad_scores = (probability * (grad_probs - delta)).astype(jnp.bfloat16)
        query_parts.append(
            scale_score
            * jnp.einsum(
                "chqk,kche->qche", grad_scores, key_rows, preferred_element_type=jnp.float32
            )
        )
        grad_keys = grad_keys + scale_score * jnp.einsum(
            "chqk,qche->kche", grad_scores, block_query, preferred_element_type=jnp.float32
        )
    grad_queries = jnp.concatenate(query_parts, axis=0)
    return jnp.stack([grad_queries, grad_keys, grad_values], axis=2).astype(jnp.bfloat16)


def per_device(
    inputs,
    teacher,
    clip_tokens,
    owners,
    qkv_master,
    out_master,
    up_master,
    down_master,
    norm_gains,
    shift_vectors,
    split_vectors,
    bases,
    first_moments,
    second_moments,
    plain_first,
    plain_second,
    split_first,
    split_second,
):
    local_rows, clips_here, model_width = inputs.shape
    group_count = lax.axis_size("mp")
    group_index = lax.axis_index("mp")
    shard_count = lax.axis_size("dp")
    shard_index = lax.axis_index("dp")
    seq_len = local_rows * group_count
    row_blocks = qkv_master.shape[0]
    shard_rows = qkv_master.shape[1]
    group_width = qkv_master.shape[3]
    group_ff = up_master.shape[2]
    head_count = group_width // HD
    block_rows = seq_len // 2
    split_row = split_vectors[0]
    query_bias = split_row[:group_width]
    value_bias = split_row[group_width : 2 * group_width]
    up_bias = split_row[2 * group_width :]
    positions = group_index * local_rows + jnp.arange(local_rows)
    row_valid = positions[:, None] < clip_tokens[None, :]
    key_valid = jnp.arange(seq_len)[None, :] < clip_tokens[:, None]
    qkv_gathered, out_gathered = (
        lax.all_gather(qkv_master.astype(jnp.bfloat16), "dp", axis=1, tiled=True),
        lax.all_gather(out_master.astype(jnp.bfloat16), "dp", axis=1, tiled=True),
    )
    qkv_weight = qkv_gathered.reshape(model_width, 3 * group_width)
    out_weight = out_gathered.reshape(group_width, model_width)
    tokens = inputs.astype(jnp.float32)
    normed_all = collect_rows(
        layer_norm(tokens, norm_gains[0], shift_vectors[0]).astype(jnp.bfloat16)
    )
    projected = jnp.einsum(
        "scd,de->sce", normed_all, qkv_weight, preferred_element_type=jnp.float32
    )
    projected = projected + jnp.concatenate([query_bias, jnp.zeros_like(query_bias), value_bias])
    proj_rows = projected.astype(jnp.bfloat16).reshape(seq_len, clips_here, 3, head_count, HD)
    attended, log_sums = attend_forward(proj_rows, key_valid, block_rows)

    def out_term(row_start, row_count):
        return jnp.einsum("scm,md->scd", attended, out_weight, preferred_element_type=jnp.float32)

    hidden = tokens + reduce_rows(out_term, local_rows) + shift_vectors[1]
    up_gathered, down_gathered = (
        lax.all_gather(up_master.astype(jnp.bfloat16), "dp", axis=1, tiled=True),
        lax.all_gather(down_master.astype(jnp.bfloat16), "dp", axis=1, tiled=True),
    )
    up_weight = up_gathered.reshape(model_width, group_ff)
    down_weight = down_gathered.reshape(group_ff, model_width)
    normed_two_all = collect_rows(
        layer_norm(hidden, norm_gains[1], shift_vectors[2]).astype(jnp.bfloat16)
    )
    upper_pre = (
        jnp.einsum("scd,df->scf", normed_two_all, up_weight, preferred_element_type=jnp.float32)
        + up_bias
    )
    active = jax.nn.gelu(upper_pre, approximate=False).astype(jnp.bfloat16)

    def down_term(row_start, row_count):
        return jnp.einsum("scf,fd->scd", active, down_weight, preferred_element_type=jnp.float32)

    final_rows = hidden + reduce_rows(down_term, local_rows) + shift_vectors[3]
    output = final_rows.astype(jnp.bfloat16)
    grad_final = jnp.where(row_valid[:, :, None], final_rows - teacher.astype(jnp.float32), 0.0)
    _, gelu_pull = jax.vjp(partial(jax.nn.gelu, approximate=False), upper_pre)
    up_again, down_again = (
        lax.all_gather(up_master.astype(jnp.bfloat16), "dp", axis=1, tiled=True),
        lax.all_gather(down_master.astype(jnp.bfloat16), "dp", axis=1, tiled=True),
    )
    up_back = up_again.reshape(model_width, group_ff)
    down_back = down_again.reshape(group_ff, model_width)
    grad_final_all = collect_rows(grad_final.astype(jnp.bfloat16))
    grad_active = jnp.einsum(
        "scd,fd->scf", grad_final_all, down_back, preferred_element_type=jnp.float32
    )
    grad_down = jnp.einsum(
        "scf,scd->fd", active, grad_final_all, preferred_element_type=jnp.float32
    )
    grad_upper = gelu_pull(grad_active)[0].astype(jnp.bfloat16)
    grad_up = jnp.einsum(
        "scd,scf->df", normed_two_all, grad_upper, preferred_element_type=jnp.float32
    )
    grad_up_bias = jnp.sum(grad_upper, axis=(0, 1), dtype=jnp.float32)

    def up_back_term(row_start, row_count):
        return jnp.einsum("scf,df->scd", grad_upper, up_back, preferred_element_type=jnp.float32)

    grad_normed_two = reduce_rows(up_back_term, local_rows)
    _, norm_two_pull = jax.vjp(layer_norm, hidden, norm_gains[1], shift_vectors[2])
    hidden_part, grad_gain_two, grad_shift_two = norm_two_pull(grad_normed_two)
    grad_hidden = grad_final + hidden_part
    qkv_again, out_again = (
        lax.all_gather(qkv_master.astype(jnp.bfloat16), "dp", axis=1, tiled=True),
        lax.all_gather(out_master.astype(jnp.bfloat16), "dp", axis=1, tiled=True),
    )
    qkv_back = qkv_again.reshape(model_width, 3 * group_width)
    out_back = out_again.reshape(group_width, model_width)
    grad_hidden_all = collect_rows(grad_hidden.astype(jnp.bfloat16))
    grad_attended = jnp.einsum(
        "scd,md->scm", grad_hidden_all, out_back, preferred_element_type=jnp.float32
    ).astype(jnp.bfloat16)
    grad_out = jnp.einsum(
        "scm,scd->md", attended, grad_hidden_all, preferred_element_type=jnp.float32
    )
    grad_proj = attend_backward(proj_rows, log_sums, grad_attended, key_valid, block_rows)
    bias_sums = jnp.sum(grad_proj, axis=(0, 1), dtype=jnp.float32)
    grad_proj_flat = grad_proj.reshape(seq_len, clips_here, 3 * group_width)
    grad_qkv = jnp.einsum(
        "scd,sce->de", normed_all, grad_proj_flat, preferred_element_type=jnp.float32
    )

    def qkv_back_term(row_start, row_count):
        return jnp.einsum(
            "sce,de->scd", grad_proj_flat, qkv_back, preferred_element_type=jnp.float32
        )

    grad_normed = reduce_rows(qkv_back_term, local_rows)
    _, norm_one_pull = jax.vjp(layer_norm, tokens, norm_gains[0], shift_vectors[0])
    tokens_part, grad_gain_one, grad_shift_one = norm_one_pull(grad_normed)
    input_grad = grad_hidden + tokens_part
    plain_local = jnp.stack(
        [
            grad_gain_one,
            grad_shift_one,
            jnp.sum(grad_hidden, axis=(0, 1)),
            grad_gain_two,
            grad_shift_two,
            jnp.sum(grad_final, axis=(0, 1)),
        ]
    )
    plain_total = lax.psum(plain_local, ("dp", "mp"))
    split_local = jnp.concatenate(
        [bias_sums[0].reshape(-1), bias_sums[2].reshape(-1), grad_up_bias]
    )[None, :]
    split_total = lax.psum(split_local, "dp")
    qkv_shard, out_shard, up_shard, down_shard = (
        lax.psum_scatter(
            grad_qkv.reshape(row_blocks, B, 3, group_width), "dp", scatter_dimension=1, tiled=True
        ),
        lax.psum_scatter(
            grad_out.reshape(group_width // B, B, model_width),
            "dp",
            scatter_dimension=1,
            tiled=True,
        ),
        lax.psum_scatter(
            grad_up.reshape(row_blocks, B, group_ff), "dp", scatter_dimension=1, tiled=True
        ),
        lax.psum_scatter(
            grad_down.reshape(group_ff // B, B, model_width), "dp", scatter_dimension=1, tiled=True
        ),
    )
    grad_blocks = jnp.concatenate(
        [
            qkv_shard.reshape(row_blocks, shard_rows, 3, group_width // B, B)
            .transpose(0, 2, 3, 1, 4)
            .reshape(-1, shard_rows, B),
            out_shard.reshape(group_width // B, shard_rows, row_blocks, B)
            .transpose(0, 2, 1, 3)
            .reshape(-1, shard_rows, B),
            up_shard.reshape(row_blocks, shard_rows, group_ff // B, B)
            .transpose(0, 2, 1, 3)
            .reshape(-1, shard_rows, B),
            down_shard.reshape(group_ff // B, shard_rows, row_blocks, B)
            .transpose(0, 2, 1, 3)
            .reshape(-1, shard_rows, B),
        ],
        axis=0,
    )
    block_count = owners.shape[0]
    cap_count = bases.shape[0]
    block_ids = jnp.arange(block_count)
    same_owner = owners[:, None] == owners[None, :]
    earlier = block_ids[None, :] < block_ids[:, None]
    slot_pos = jnp.sum((same_owner & earlier).astype(jnp.int32), axis=1)
    select = (
        (slot_pos[None, None, :] == jnp.arange(cap_count)[:, None, None])
        & (owners[None, None, :] == jnp.arange(shard_count)[None, :, None])
    ).astype(jnp.float32)
    outgoing = jnp.einsum("cjk,krb->cjrb", select, grad_blocks, precision=highest)
    incoming = (
        lax.all_to_all(outgoing.astype(jnp.bfloat16), "dp", split_axis=1, concat_axis=1, tiled=True)
        .astype(outgoing.dtype)
        .reshape(cap_count, B, B)
    )
    slot_used = jnp.any(
        (owners[None, :] == shard_index) & (slot_pos[None, :] == jnp.arange(cap_count)[:, None]),
        axis=1,
    )
    old_first = first_moments[:, 0]
    old_second = second_moments[:, 0]
    new_first, new_second, update = rotate_adam(
        incoming, bases[:, 0, 0], bases[:, 0, 1], old_first, old_second
    )
    first_new = jnp.where(slot_used[:, None, None], new_first, old_first)[:, None]
    second_new = jnp.where(slot_used[:, None, None], new_second, old_second)[:, None]
    returned = lax.all_to_all(
        update.reshape(cap_count, shard_count, shard_rows, B).astype(jnp.bfloat16),
        "dp",
        split_axis=1,
        concat_axis=1,
        tiled=True,
    ).astype(jnp.float32)
    picked = jnp.take(
        returned.reshape(cap_count * shard_count, shard_rows, B),
        slot_pos * shard_count + owners,
        axis=0,
    )
    count_qkv = row_blocks * 3 * (group_width // B)
    count_out = group_width // B * row_blocks
    count_up = row_blocks * (group_ff // B)
    qkv_update = (
        picked[:count_qkv]
        .reshape(row_blocks, 3, group_width // B, shard_rows, B)
        .transpose(0, 3, 1, 2, 4)
        .reshape(row_blocks, shard_rows, 3, group_width)
    )
    out_update = (
        picked[count_qkv : count_qkv + count_out]
        .reshape(group_width // B, row_blocks, shard_rows, B)
        .transpose(0, 2, 1, 3)
        .reshape(group_width // B, shard_rows, model_width)
    )
    up_update = (
        picked[count_qkv + count_out : count_qkv + count_out + count_up]
        .reshape(row_blocks, group_ff // B, shard_rows, B)
        .transpose(0, 2, 1, 3)
        .reshape(row_blocks, shard_rows, group_ff)
    )
    down_update = (
        picked[count_qkv + count_out + count_up :]
        .reshape(group_ff // B, row_blocks, shard_rows, B)
        .transpose(0, 2, 1, 3)
        .reshape(group_ff // B, shard_rows, model_width)
    )
    qkv_new = qkv_master - rate_qkv * qkv_update
    out_new = out_master - rate_out * out_update
    up_new = up_master - rate_up * up_update
    down_new = down_master - rate_down * down_update
    plain_param = jnp.stack(
        [
            norm_gains[0],
            shift_vectors[0],
            shift_vectors[1],
            norm_gains[1],
            shift_vectors[2],
            shift_vectors[3],
        ]
    )
    plain_new, plain_first_new, plain_second_new = adam_rows(
        plain_total, plain_param, plain_first, plain_second
    )
    gains_new = jnp.stack([plain_new[0], plain_new[3]])
    shifts_new = jnp.stack([plain_new[1], plain_new[2], plain_new[4], plain_new[5]])
    split_new, split_first_new, split_second_new = adam_rows(
        split_total, split_vectors, split_first, split_second
    )
    return (
        output,
        input_grad,
        qkv_new,
        out_new,
        up_new,
        down_new,
        qkv_new.astype(jnp.bfloat16),
        out_new.astype(jnp.bfloat16),
        up_new.astype(jnp.bfloat16),
        down_new.astype(jnp.bfloat16),
        gains_new,
        shifts_new,
        split_new,
        first_new,
        second_new,
        plain_first_new,
        plain_second_new,
        split_first_new,
        split_second_new,
    )


def solution(mesh):
    placed = (
        P("mp", "dp", None),
        P("mp", "dp", None),
        P("dp"),
        P(),
        P(None, "dp", None, "mp"),
        P("mp", "dp", None),
        P(None, "dp", "mp"),
        P("mp", "dp", None),
        P(),
        P(),
        P("mp", None),
        P("dp", "mp", None, None, None),
        P("dp", "mp", None, None),
        P("dp", "mp", None, None),
        P(),
        P(),
        P("mp", None),
        P("mp", None),
    )
    return jax.shard_map(
        per_device,
        mesh=mesh,
        in_specs=placed,
        out_specs=(
            P("mp", "dp", None),
            P("mp", "dp", None),
            P(None, "dp", None, "mp"),
            P("mp", "dp", None),
            P(None, "dp", "mp"),
            P("mp", "dp", None),
            P(None, "dp", None, "mp"),
            P("mp", "dp", None),
            P(None, "dp", "mp"),
            P("mp", "dp", None),
            P(),
            P(),
            P("mp", None),
            P("dp", "mp", None, None),
            P("dp", "mp", None, None),
            P(),
            P(),
            P("mp", None),
            P("mp", None),
        ),
        check_vma=False,
    )
```

profile of v0, /device:TPU:0, one launch (start us, length us, event | category | flops | bytes accessed | tf_op | source)
XLA Modules:
  0.0 1609.1 jit_solution(378699572807345866)
XLA Ops:
  41.7 117.6 %all-gather.8.cloned.1.call-done = bf16[1568,2,1024]{2,0,1:T(8,128)(2,1)} async-done(((bf16[392,2,1024]{2,0,1:T(8,128)(2,1)}), bf16[1568,2,1024]{2,0,1:T(8,128)(2,1)}) %all-gather.8.cloned.1.call-update) | async-done | bytes 6422544 | tf_op jit(solution)/shard_map/all_gather | solution.py:57
  176.6 18.2 %fusion.127 = (f32[2,4,784]{2,1,0:T(4,128)S(1)}, f32[2,4,784,1568]{3,2,1,0:T(8,128)}) fusion(bf16[1568,2,3,4,64]{0,4,3,2,1:T(8,128)(2,1)} %bitcast.365, pred[2,1568]{1,0:T(4,128)(4,1)S(1)} %iota_compare_fusion.2), kind=kOutput, calls=%fused_computation.238 | convolution fusion | flops 1288312704 | bytes 41987648 | tf_op jit(solution)/shard_map/qche,kche->chqk/dot_general | solution.py:71
  194.8 16.5 %fusion.128 = (f32[2,4,784]{2,1,0:T(4,128)S(1)}, f32[2,4,784,1568]{3,2,1,0:T(8,128)}) fusion(bf16[1568,2,3,4,64]{0,4,3,2,1:T(8,128)(2,1)S(1)} %bitcast.368, pred[2,1568]{1,0:T(4,128)(4,1)S(1)} %iota_compare_fusion.2), kind=kOutput, calls=%fused_computation.239 | convolution fusion | flops 1288312704 | bytes 41991168 | tf_op jit(solution)/shard_map/qche,kche->chqk/dot_general | solution.py:71
  242.4 15.7 fusion
  282.1 109.4 %reduce-scatter.25.cloned.1.call-done = bf16[392,2048]{1,0:T(8,128)(2,1)} async-done(((bf16[1568,2048]{1,0:T(8,128)(2,1)}), bf16[392,2048]{1,0:T(8,128)(2,1)}) %reduce-scatter.25.cloned.1.call-update) | async-done | bytes 1605648
  398.6 23.6 %all-gather.14.cloned.1.call-done = bf16[8,128,1024]{2,1,0:T(8,128)(2,1)} async-done(((bf16[8,16,1024]{2,1,0:T(8,128)(2,1)}), bf16[8,128,1024]{2,1,0:T(8,128)(2,1)}) %all-gather.14.cloned.1.call-update) | async-done | bytes 2097168 | tf_op jit(solution)/shard_map/all_gather | solution.py:198
  422.2 119.5 %all-gather.12.cloned.1.call-done = bf16[1568,2,1024]{2,0,1:T(8,128)(2,1)} async-done(((bf16[392,2,1024]{2,0,1:T(8,128)(2,1)}), bf16[1568,2,1024]{2,0,1:T(8,128)(2,1)}) %all-gather.12.cloned.1.call-update) | async-done | bytes 6422544 | tf_op jit(solution)/shard_map/all_gather | solution.py:57
  541.7 18.4 %fusion.39 = (u8[1568,1024]{1,0:T(8,128)(4,1)S(1)}, u8[1568,1024]{1,0:T(8,128)(4,1)S(1)}, f32[1568,2,1024]{2,0,1:T(8,128)}) fusion(f32[1024]{0:T(1024)S(1)} %bitcast.458, bf16[1568,2,1024]{2,0,1:T(8,128)(2,1)} %all-gather.12.cloned.1.call-done, bf16[1024,1024,1]{1,0,2:T(8,128)(2,1)} %bitcast.469), kind=kOutput, calls=%fused_computation.94 | convolution fusion | flops 6618415104 | bytes 24580096 | tf_op jit(solution)/shard_map/scd,df->scf/dot_general | solution.py:207
  560.0 32.8 %multiply_convert_fusion.2 = (bf16[1568,2,1024]{2,0,1:T(8,128)(2,1)}, f32[1568,2,1024]{2,0,1:T(8,128)}) fusion(f32[1568,2,1024]{2,0,1:T(8,128)} %get-tuple-element.197, f32[1024]{0:T(1024)S(1)} %bitcast.459, u8[1568,1024]{1,0:T(8,128)(4,1)S(1)} %get-tuple-element.134, u8[1568,1024]{1,0:T(8,128)(4,1)S(1)} %get-tuple-element.133), kind=kLoop, calls=%fused_computation.32 | loop fusion | flops 227999744 | bytes 35328000 | tf_op jit(solution)/shard_map/convert_element_type | solution.py:210
  607.2 110.3 %reduce-scatter.27.cloned.1.call-done = bf16[392,2048]{1,0:T(8,128)(2,1)} async-done(((bf16[1568,2048]{1,0:T(8,128)(2,1)}), bf16[392,2048]{1,0:T(8,128)(2,1)}) %reduce-scatter.27.cloned.1.call-update) | async-done | bytes 1605648
  725.6 118.1 %all-gather.18.cloned.1.call-done = bf16[1568,2,1024]{2,0,1:T(8,128)(2,1)} async-done(((bf16[392,2,1024]{2,0,1:T(8,128)(2,1)}), bf16[1568,2,1024]{2,0,1:T(8,128)(2,1)}) %all-gather.18.cloned.1.call-update) | async-done | bytes 6422544 | tf_op jit(solution)/shard_map/all_gather | solution.py:57
  843.7 20.2 %convert_reduce_fusion = (f32[1024]{0:T(1024)}, bf16[1568,2,1024]{2,0,1:T(8,128)(2,1)}) fusion(f32[1568,2,1024]{2,0,1:T(8,128)} %get-tuple-element.166, bf16[1568,2,1024]{2,0,1:T(8,128)(2,1)} %all-gather.18.cloned.1.call-done, bf16[1024,1024,1]{1,0,2:T(8,128)(2,1)} %bitcast.472, f32[1568,2,1024]{2,0,1:T(8,128)} %get-tuple-element.197, f32[1024]{0:T(1024)S(1)} %bitcast.460), kind=kOutput, calls=%fused_computation.30 | convolution fusion | flops 6631259136 | bytes 40640512 | tf_op jit(solution)/shard_map/scd,fd->scf/dot_general | solution.py:226
  877.9 111.0 %reduce-scatter.29.cloned.1.call-done = bf16[392,2048]{1,0:T(8,128)(2,1)} async-done(((bf16[1568,2048]{1,0:T(8,128)(2,1)}), bf16[392,2048]{1,0:T(8,128)(2,1)}) %reduce-scatter.29.cloned.1.call-update) | async-done | bytes 1605648
  1032.4 86.6 %all-gather.20.cloned.1.call-done = bf16[1568,2,1024]{2,0,1:T(8,128)(2,1)} async-done(((bf16[392,2,1024]{2,0,1:T(8,128)(2,1)}), bf16[1568,2,1024]{2,0,1:T(8,128)(2,1)}) %all-gather.20.cloned.1.call-update) | async-done | bytes 6422544 | tf_op jit(solution)/shard_map/all_gather | solution.py:57
  1125.5 30.2 %multiply_reduce_fusion.1 = (f32[2,4,784]{2,1,0:T(4,128)S(1)}, f32[2,4,784,1568]{3,2,1,0:T(8,128)}) fusion(f32[2,4,784,1568]{3,2,1,0:T(8,128)} %get-tuple-element.196, f32[2,4,784]{2,1,0:T(4,128)S(1)} %bitcast.411, bf16[784,2,4,64]{0,3,2,1:T(8,128)(2,1)S(1)} %bitcast.399, bf16[1568,2,3,4,64]{0,4,3,2,1:T(8,128)(2,1)} %bitcast.366), kind=kOutput, calls=%fused_computation.5 | convolution fusion | flops 1288312704 | bytes 83641344 | tf_op jit(solution)/shard_map/qche,kche->chqk/dot_general | solution.py:119
  1155.8 36.3 %multiply_convert_fusion.1 = bf16[2,4,784,1568]{3,2,1,0:T(8,128)(2,1)} fusion(f32[2,4,784,1568]{3,2,1,0:T(8,128)} %get-tuple-element.199, f32[2,4,784,1568]{3,2,1,0:T(8,128)} %get-tuple-element.196, f32[2,4,784]{2,1,0:T(4,128)S(1)} %get-tuple-element.198, f32[2,4,784]{2,1,0:T(4,128)S(1)} %bitcast.412), kind=kLoop, calls=%fused_computation.4 | loop fusion | flops 39337984 | bytes 98395136 | tf_op jit(solution)/shard_map/convert_element_type | solution.py:123
  1218.4 29.9 %multiply_reduce_fusion = (f32[2,4,784]{2,1,0:T(4,128)S(1)}, f32[2,4,784,1568]{3,2,1,0:T(8,128)}) fusion(f32[2,4,784,1568]{3,2,1,0:T(8,128)} %get-tuple-element.194, f32[2,4,784]{2,1,0:T(4,128)} %bitcast.414, bf16[784,2,4,64]{0,3,2,1:T(8,128)(2,1)S(1)} %bitcast.401, bf16[1568,2,3,4,64]{0,4,3,2,1:T(8,128)(2,1)} %bitcast.367), kind=kOutput, calls=%fused_computation.2 | convolution fusion | flops 1288312704 | bytes 83644928 | tf_op jit(solution)/shard_map/qche,kche->chqk/dot_general | solution.py:119
  1248.3 33.8 %multiply_convert_fusion = bf16[2,4,784,1568]{3,2,1,0:T(8,128)(2,1)} fusion(f32[2,4,784,1568]{3,2,1,0:T(8,128)} %get-tuple-element.201, f32[2,4,784,1568]{3,2,1,0:T(8,128)} %get-tuple-element.194, f32[2,4,784]{2,1,0:T(4,128)S(1)} %get-tuple-element.200, f32[2,4,784]{2,1,0:T(4,128)S(1)} %bitcast.415), kind=kLoop, calls=%fused_computation.1 | loop fusion | flops 39337984 | bytes 98395136 | tf_op jit(solution)/shard_map/convert_element_type | solution.py:123
  1313.6 16.4 %fusion.4 = f32[2,4,64,1568]{3,2,1,0:T(8,128)S(1)} fusion(bf16[784,2,4,64]{0,3,2,1:T(8,128)(2,1)} %bitcast.402, f32[2,4,784,1568]{3,2,1,0:T(8,128)} %get-tuple-element.194, f32[2,4,784]{2,1,0:T(4,128)S(1)} %bitcast.416), kind=kOutput, calls=%fused_computation.17 | convolution fusion | flops 1278484480 | bytes 43377152 | tf_op jit(solution)/shard_map/chqk,qche->kche/dot_general | solution.py:113
  1330.0 17.8 %add_bitcast_fusion = bf16[1568,2,1,4,64]{0,4,3,1,2:T(8,128)(2,1)} fusion(f32[2,4,64,1568]{3,2,1,0:T(8,128)S(1)} %fusion.4, bf16[784,2,4,64]{0,3,2,1:T(8,128)(2,1)} %bitcast.400, f32[2,4,784,1568]{3,2,1,0:T(8,128)} %get-tuple-element.196, f32[2,4,784]{2,1,0:T(4,128)S(1)} %bitcast.413), kind=kOutput, calls=%fused_computation.77 | convolution fusion | flops 1280090112 | bytes 44982784 | tf_op jit(solution)/shard_map/chqk,qche->kche/dot_general | solution.py:113
  1383.3 48.9 %reduce-scatter.17.cloned.1.call-done = f32[8,16,3,256]{3,1,2,0:T(8,128)} async-done(((f32[8,128,3,256]{3,1,2,0:T(8,128)}), f32[8,16,3,256]{3,1,2,0:T(8,128)}) %reduce-scatter.17.cloned.1.call-update) | async-done | bytes 393232 | tf_op jit(solution)/shard_map/reduce_scatter | solution.py:290
  1443.9 17.1 %all-to-all-done = bf16[48,8,16,128]{3,2,0,1:T(8,128)(2,1)S(1)} async-done(((bf16[48,8,16,128]{3,2,0,1:T(8,128)(2,1)}), bf16[48,8,16,128]{3,2,0,1:T(8,128)(2,1)S(1)}, u32[]{:S(2)}, u32[]{:S(2)}) %all-to-all-start) | async-done | bytes 1572896 | tf_op jit(solution)/shard_map/all_to_all | solution.py:335
  1490.2 28.5 %psum.15 = f32[1,1536]{1,0:T(1,128)S(1)} all-reduce(f32[1,1536]{1,0:T(1,128)S(1)} %broadcast_in_dim.138), channel_id=1, replica_groups=mesh['dp'=8,'mp'=4] {'dp'}, use_global_device_ids=true, to_apply=%region_34.35 | all-reduce | flops 1536 | bytes 12288 | tf_op jit(solution)/shard_map/psum | solution.py:288
  1552.3 40.9 %psum.14 = f32[6,1024]{1,0:T(8,128)S(1)} all-reduce(f32[6,1024]{1,0:T(8,128)S(1)} %stack.55), channel_id=1, replica_groups=mesh['dp'=8,'mp'=4] {'dp','mp'}, use_global_device_ids=true, to_apply=%region_30.31 | all-reduce | flops 6144 | bytes 49152 | tf_op jit(solution)/shard_map/psum | solution.py:284
  (314 shorter events, 375.5 us)
Async XLA Ops:
  7.2 32.5 %all-gather.10.cloned.1.call-start = ((), (), s32[]{:S(2)}) async-start(), calls=%async_computation.11 | async-start | bytes 1769472 | tf_op jit(solution)/shard_map/all_gather | solution.py:177
  9.1 150.3 %all-gather.8.cloned.1.call-start = ((), (), s32[]{:S(2)}) async-start(), calls=%async_computation.10 | async-start | bytes 8028160 | tf_op jit(solution)/shard_map/all_gather | solution.py:57
  15.5 376.0 %reduce-scatter.25.cloned.1.call-start = ((), (), s32[]{:S(2)}) async-start(), calls=%async_computation.21 | async-start | bytes 8028160
  41.7 127.4 %copy-start.27 = (bf16[8,128,3,256]{1,0,3,2:T(8,128)(2,1)}, bf16[8,128,3,256]{1,0,3,2:T(8,128)(2,1)S(1)}, u32[]{:S(2)}) copy-start(bf16[8,128,3,256]{1,0,3,2:T(8,128)(2,1)S(1)} %copy.205) | copy-start | bytes 4718596
  280.2 111.3 %copy-start.1 = (bf16[392,2,1024]{2,1,0:T(2,128)(2,1)S(1)}, bf16[392,2,1024]{2,1,0:T(2,128)(2,1)}, u32[]{:S(2)}) copy-start(bf16[392,2,1024]{2,1,0:T(2,128)(2,1)} %param.18) | copy-start | bytes 4816900
  280.2 111.3 %copy-start.32 = (f32[1,1024]{1,0:T(1,128)S(1)}, f32[1,1024]{1,0:T(1,128)}, u32[]{:S(2)}) copy-start(f32[1,1024]{1,0:T(1,128)} %get-tuple-element.183) | copy-start | bytes 12292
  280.2 141.9 %all-gather.14.cloned.1.call-start = ((), (), s32[]{:S(2)}) async-start(), calls=%async_computation.13 | async-start | bytes 2359296 | tf_op jit(solution)/shard_map/all_gather | solution.py:198
  282.0 259.6 %all-gather.12.cloned.1.call-start = ((), (), s32[]{:S(2)}) async-start(), calls=%async_computation.12 | async-start | bytes 8028160 | tf_op jit(solution)/shard_map/all_gather | solution.py:57
  396.6 196.2 %all-gather.16.cloned.1.call-start = ((), (), s32[]{:S(2)}) async-start(), calls=%async_computation.14 | async-start | bytes 2359296 | tf_op jit(solution)/shard_map/all_gather | solution.py:199
  398.5 319.0 %reduce-scatter.27.cloned.1.call-start = ((), (), s32[]{:S(2)}) async-start(), calls=%async_computation.22 | async-start | bytes 8028160
  606.5 111.0 %copy-start.54 = (f32[1,1024]{1,0:T(1,128)S(1)}, f32[1,1024]{1,0:T(1,128)}, u32[]{:S(2)}) copy-start(f32[1,1024]{1,0:T(1,128)} %get-tuple-element.181) | copy-start | bytes 12292
  606.5 237.2 %all-gather.18.cloned.1.call-start = ((), (), s32[]{:S(2)}) async-start(), calls=%async_computation.15 | async-start | bytes 8028160 | tf_op jit(solution)/shard_map/all_gather | solution.py:57
  725.5 263.4 %reduce-scatter.29.cloned.1.call-start = ((), (), s32[]{:S(2)}) async-start(), calls=%async_computation.23 | async-start | bytes 8028160
  877.7 241.3 %all-gather.20.cloned.1.call-start = ((), (), s32[]{:S(2)}) async-start(), calls=%async_computation.16 | async-start | bytes 8028160 | tf_op jit(solution)/shard_map/all_gather | solution.py:57
  1000.9 376.8 %reduce-scatter.23.cloned.1.call-start = ((), (), s32[]{:S(2)}) async-start(), calls=%async_computation.20 | async-start | bytes 4718592 | tf_op jit(solution)/shard_map/reduce_scatter | solution.py:302
  1013.6 365.3 %reduce-scatter.21.cloned.1.call-start = ((), (), s32[]{:S(2)}) async-start(), calls=%async_computation.19 | async-start | bytes 4718592 | tf_op jit(solution)/shard_map/reduce_scatter | solution.py:299
  1032.4 86.6 %copy-start.26 = (bf16[2,128,1024]{2,1,0:T(8,128)(2,1)S(1)}, bf16[2,128,1024]{2,1,0:T(8,128)(2,1)}, u32[]{:S(2)}) copy-start(bf16[2,128,1024]{2,1,0:T(8,128)(2,1)} %all_gather.30) | copy-start | bytes 1572868
  1032.4 350.0 %reduce-scatter.19.cloned.1.call-start = ((), (), s32[]{:S(2)}) async-start(), calls=%async_computation.18 | async-start | bytes 1179648 | tf_op jit(solution)/shard_map/reduce_scatter | solution.py:293
  1125.5 66.6 %slice-start = ((s8[5111808]{0:T(1024)(128)(4,1)}), s8[4194304]{0:T(1024)(128)(4,1)S(1)}, s32[]{:S(2)}) async-start(s8[5111808]{0:T(1024)(128)(4,1)} %bitcast.371), calls=%async_computation.25 | async-start | bytes 8388608
  1218.4 63.7 %slice-start.2 = ((s8[5111808]{0:T(1024)(128)(4,1)}), s8[4194304]{0:T(1024)(128)(4,1)S(1)}, s32[]{:S(2)}) async-start(s8[5111808]{0:T(1024)(128)(4,1)} %bitcast.375), calls=%async_computation.27 | async-start | bytes 8388608
  1347.8 84.4 %reduce-scatter.17.cloned.1.call-start = ((), (), s32[]{:S(2)}) async-start(), calls=%async_computation.17 | async-start | bytes 3538944 | tf_op jit(solution)/shard_map/reduce_scatter | solution.py:290
  1364.0 183.3 %reduce-scatter.31.cloned.1.call-start = ((), (), s32[]{:S(2)}) async-start(), calls=%async_computation.24 | async-start | bytes 8028160
  1436.5 24.5 %all-to-all-start = ((bf16[48,8,16,128]{3,2,0,1:T(8,128)(2,1)}), bf16[48,8,16,128]{3,2,0,1:T(8,128)(2,1)S(1)}, u32[]{:S(2)}, u32[]{:S(2)}) async-start(bf16[48,8,16,128]{3,2,0,1:T(8,128)(2,1)} %copy.226), calls=%async_computation.4 | async-start | bytes 3145728 | tf_op jit(solution)/shard_map/all_to_all | solution.py:335
  1485.7 42.2 %all-to-all-start.1 = ((bf16[48,8,16,128]{3,2,0,1:T(8,128)(2,1)}), bf16[48,8,16,128]{3,2,0,1:T(8,128)(2,1)}, u32[]{:S(2)}, u32[]{:S(2)}) async-start(bf16[48,8,16,128]{3,2,0,1:T(8,128)(2,1)} %copy.234), calls=%async_computation.5 | async-start | bytes 3145728 | tf_op jit(solution)/shard_map/all_to_all | solution.py:350
  (67 other events, 726.2 us)
Sparse Core Ops, SparseCore 0:
  10.5 29.1 all-gather.9
  41.9 117.4 all-gather.7
  280.4 111.0 reduce-scatter.24
  393.8 28.2 all-gather.13
  424.1 117.4 all-gather.11
  544.0 25.9 all-gather.15
  606.6 110.8 reduce-scatter.26
  725.7 117.9 all-gather.17
  877.8 111.0 reduce-scatter.28
  1001.0 117.9 all-gather.19
  1122.4 49.2 reduce-scatter.22
  1174.9 51.0 reduce-scatter.20
  1348.0 34.3 reduce-scatter.18
  1386.2 46.0 reduce-scatter.16
  1434.4 112.8 reduce-scatter.30
where the time goes:
time: 1610 us
  waiting for transfers between devices  884 us (55%)
  matrix products  352 us (22%)
  other arithmetic  196 us (12%)
  blocking collectives  82.8 us (5%)
  local copies, waits for them, and re-layouts  70 us (4%)
    all_gather x4, waiting for transfers between devices, collect_rows(): return lax.all_gather(values, 'mp', axis=0, tiled=True)  442 us
    unnamed x19, waiting for transfers between devices  340 us
    convert_element_type x2, other arithmetic, attend_backward(): grad_scores = (probability * (grad_probs - delta)).astype(jnp.bfloat16)  70.1 us
    dot_general x2, matrix products, attend_backward(): jnp.einsum('qche,kche->chqk', block_grad, value_rows, preferred_element_t...  60.1 us
    reduce_scatter x1, waiting for transfers between devices, per_device(): lax.psum_scatter(grad_qkv.reshape(row_blocks, B, 3, group_width), 'dp', s...  48.9 us
    unnamed x158, local copies, waits for them, and re-layouts  43.5 us
    psum x1, blocking collectives, per_device(): plain_total = lax.psum(plain_local, ('dp', 'mp'))  40.9 us
    dot_general x2, matrix products, masked_scores(): jnp.einsum('qche,kche->chqk', block_query, key_rows, preferred_element_ty...  34.7 us
  transfers between devices with their start and end apart: 17, of which 13 were waited for; matrix products, arithmetic and copies ran while one was open for 25% of the time, Pallas kernels for 0%

commit v1 on v0

v1 whole, which is shorter than its diff:
```python
from functools import partial

import jax
import jax.numpy as jnp
from jax import lax
from jax.experimental import pallas as pl
from jax.experimental.pallas import tpu as pltpu
from jax.sharding import PartitionSpec as P

HD = 64
B = 128
PAIR = 2 * HD


eps_norm = 1e-06
eps_adam = 1e-08
beta_first = 0.5
beta_second = 0.6
rate_qkv = 0.016
rate_out = 0.25
rate_up = 0.016
rate_down = 0.008
rate_vector = 0.3
scale_score = 0.125

f32 = jnp.float32
bf16 = jnp.bfloat16
NT = (((1,), (1,)), ((), ()))
NN = (((1,), (0,)), ((), ()))
TN = (((0,), (0,)), ((), ()))


def dot(left, right, dims=NN):
    return lax.dot_general(left, right, dims, preferred_element_type=f32)


def layer_norm(values, scale_row, shift_row):
    average = jnp.mean(values, axis=-1, keepdims=True)
    centered = values - average
    variance = jnp.mean(centered * centered, axis=-1, keepdims=True)
    return centered * lax.rsqrt(variance + 1e-06) * scale_row + shift_row


def adam_rows(grad_rows, param_rows, first_rows, second_rows):
    scaled = grad_rows * lax.rsqrt(
        jnp.mean(grad_rows * grad_rows, axis=-1, keepdims=True) + eps_norm
    )
    new_first = beta_first * first_rows + (1.0 - beta_first) * scaled
    new_second = beta_second * second_rows + (1.0 - beta_second) * scaled * scaled
    step_rows = new_first / (jnp.sqrt(new_second) + eps_adam)
    return (param_rows - rate_vector * step_rows, new_first, new_second)


def rotate_adam(grad_blocks, left_basis, right_basis, old_first, old_second):
    high = lax.Precision.HIGH
    scaled = grad_blocks * lax.rsqrt(
        jnp.mean(grad_blocks * grad_blocks, axis=(1, 2), keepdims=True) + eps_norm
    )
    rotated = jnp.einsum("kba,kbd->kad", left_basis, scaled, precision=high)
    rotated = jnp.einsum("kad,kde->kae", rotated, right_basis, precision=high)
    new_first = beta_first * old_first + (1.0 - beta_first) * rotated
    new_second = beta_second * old_second + (1.0 - beta_second) * rotated * rotated
    step_rot = new_first / (jnp.sqrt(new_second) + eps_adam)
    update = jnp.einsum("kab,kbd->kad", left_basis, step_rot, precision=high)
    update = jnp.einsum("kad,ked->kae", update, right_basis, precision=high)
    return (new_first, new_second, update)


def lane_index(rows):
    return lax.broadcasted_iota(jnp.int32, (rows, PAIR), 1)


def own_lanes(lane, head):
    return lane < HD if head == 0 else lane >= HD


def key_operands(keys, first_row, valid):
    rows = keys.shape[0]
    lane = lane_index(rows)
    row = lax.broadcasted_iota(jnp.int32, (rows, PAIR), 0) + first_row
    wide = keys.astype(f32)
    padding = jnp.where(row >= valid, -1e30, 0.0)
    operands = []
    for head in range(2):
        base = HD * (1 - head)
        other = jnp.where(lane < base + 3, 1.0, jnp.where(lane == base + 3, padding, 0.0))
        operands.append(jnp.where(own_lanes(lane, head), wide, other).astype(bf16))
    return operands


def forward_kernel(chunk, valid_ref, q_ref, k_ref, v_ref, out_ref, log_ref, key_ref, score_ref):
    tokens = q_ref.shape[0]
    lane = lane_index(tokens)
    queries = q_ref[...].astype(f32) * scale_score
    ones = jnp.ones((16, chunk), f32)
    starts = range(0, tokens, chunk)
    outputs, logs = [], []
    for head, operand in enumerate(key_operands(k_ref[...], 0, valid_ref[0])):
        mark = jnp.where(lane == HD * (1 - head) + 3, 1.0, 0.0)
        query = jnp.where(own_lanes(lane, head), queries, mark).astype(bf16)
        key_ref[head] = operand
        top = None
        for at in starts:
            scores = dot(key_ref[head, at : at + chunk], query, NT)
            score_ref[head, at : at + chunk] = scores
            peak = jnp.max(scores, axis=0, keepdims=True)
            top = peak if top is None else jnp.maximum(top, peak)
        total = None
        for at in starts:
            turned = jnp.transpose(v_ref[at : at + chunk].astype(f32))
            values = jnp.concatenate([turned[HD * head : HD * head + HD], ones], axis=0)
            weight = jnp.exp(score_ref[head, at : at + chunk] - top).astype(bf16)
            term = dot(values.astype(bf16), weight)
            total = term if total is None else total + term
        weight_sum = total[HD : HD + 1]
        outputs.append(total[:HD] / weight_sum)
        logs.append(-(top + jnp.log(weight_sum)))
    out_ref[...] = jnp.transpose(jnp.concatenate(outputs, axis=0)).astype(bf16)
    column = jnp.ones((HD, 1), f32)
    log_ref[...] = jnp.transpose(jnp.concatenate([column * logs[1], column * logs[0]], axis=0))


def attend_forward(proj, valid, first_pair, pairs, chunk):
    tokens = proj.shape[0]
    per_part = proj.shape[1] // 3 // PAIR

    def pair_spec(at):
        return pl.BlockSpec((tokens, PAIR), lambda pair: (0, at + pair))

    return pl.pallas_call(
        partial(forward_kernel, chunk),
        grid=(pairs,),
        in_specs=[
            pl.BlockSpec(memory_space=pltpu.SMEM),
            pair_spec(first_pair),
            pair_spec(per_part + first_pair),
            pair_spec(2 * per_part + first_pair),
        ],
        out_specs=[pair_spec(0), pair_spec(0)],
        out_shape=[
            jax.ShapeDtypeStruct((tokens, pairs * PAIR), bf16),
            jax.ShapeDtypeStruct((tokens, pairs * PAIR), f32),
        ],
        scratch_shapes=[
            pltpu.VMEM((2, tokens, PAIR), bf16),
            pltpu.VMEM((2, tokens, tokens), f32),
        ],
        compiler_params=pltpu.CompilerParams(
            dimension_semantics=("arbitrary",), vmem_limit_bytes=58 * 2**20
        ),
        cost_estimate=pl.CostEstimate(
            flops=16 * pairs * tokens * tokens * PAIR,
            bytes_accessed=pairs * tokens * PAIR * 12,
            transcendentals=pairs * 2 * tokens * tokens,
        ),
    )(valid, proj, proj, proj)


def backward_kernel(
    valid_ref,
    q_ref,
    k_ref,
    v_ref,
    grad_ref,
    out_ref,
    log_ref,
    dq_ref,
    dk_ref,
    dv_ref,
    query_ref,
    cot_ref,
    turned_ref,
):
    step = pl.program_id(1)
    rows = k_ref.shape[0]
    lane = lane_index(q_ref.shape[0])

    @pl.when(step == 0)
    def _():
        queries = q_ref[...].astype(f32) * scale_score
        logs = log_ref[...]
        log_high = logs.astype(bf16).astype(f32)
        log_rest = logs - log_high
        log_middle = log_rest.astype(bf16).astype(f32)
        log_low = log_rest - log_middle
        grad = grad_ref[...].astype(f32)
        product = grad * out_ref[...].astype(f32)
        product_high = product.astype(bf16)
        product_low = (product - product_high.astype(f32)).astype(bf16)
        source = lax.broadcasted_iota(jnp.int32, (PAIR, PAIR), 0)
        target = lax.broadcasted_iota(jnp.int32, (PAIR, PAIR), 1)
        place = jnp.where((source < HD) != (target < HD), -1.0, 0.0).astype(bf16)
        delta = dot(product_high, place) + dot(product_low, place)
        delta_high = delta.astype(bf16).astype(f32)
        delta_low = delta - delta_high
        for head in range(2):
            base = HD * (1 - head)
            mine = own_lanes(lane, head)
            mark = jnp.where(lane == base + 3, 1.0, 0.0)
            other = jnp.where(lane == base + 2, log_low, mark)
            other = jnp.where(lane == base + 1, log_middle, other)
            other = jnp.where(lane == base, log_high, other)
            query_ref[head] = jnp.where(mine, queries, other).astype(bf16)
            other = jnp.where(lane == base + 1, delta_low, 0.0)
            other = jnp.where(lane == base, delta_high, other)
            cot_ref[head] = jnp.where(mine, grad, other).astype(bf16)
        turned_ref[...] = jnp.zeros_like(turned_ref)

    operands = key_operands(k_ref[...], step * rows, valid_ref[0])
    key_lane = lane_index(rows)
    wide_values = v_ref[...].astype(f32)
    turned_keys = jnp.transpose(k_ref[...].astype(f32)).astype(bf16)
    dk, dv = [], []
    for head in range(2):
        base = HD * (1 - head)
        span = slice(HD * head, HD * head + HD)
        pair_of_ones = jnp.where((key_lane == base) | (key_lane == base + 1), 1.0, 0.0)
        values = jnp.where(own_lanes(key_lane, head), wide_values, pair_of_ones).astype(bf16)
        weight = jnp.exp(dot(operands[head], query_ref[head], NT))
        slope = (weight * dot(values, cot_ref[head], NT)).astype(bf16)
        dv.append(dot(weight.astype(bf16), cot_ref[head]))
        dk.append(dot(slope, query_ref[head]))
        turned_ref[span] += dot(turned_keys[span], slope)
    dk_ref[...] = jnp.where(key_lane < HD, dk[0], dk[1]).astype(bf16)
    dv_ref[...] = jnp.where(key_lane < HD, dv[0], dv[1]).astype(bf16)

    @pl.when(step == pl.num_programs(1) - 1)
    def _():
        dq_ref[...] = (jnp.transpose(turned_ref[...]) * scale_score).astype(bf16)


def attend_backward(proj, grad, attended, logs, valid, first_pair, pairs, row_block):
    tokens = proj.shape[0]
    per_part = proj.shape[1] // 3 // PAIR

    def whole(at):
        return pl.BlockSpec((tokens, PAIR), lambda pair, step: (0, at + pair))

    def block(at):
        return pl.BlockSpec((row_block, PAIR), lambda pair, step: (step, at + pair))

    return pl.pallas_call(
        backward_kernel,
        grid=(pairs, tokens // row_block),
        in_specs=[
            pl.BlockSpec(memory_space=pltpu.SMEM),
            whole(first_pair),
            block(per_part + first_pair),
            block(2 * per_part + first_pair),
            whole(0),
            whole(0),
            whole(0),
        ],
        out_specs=[whole(0), block(0), block(0)],
        out_shape=[jax.ShapeDtypeStruct((tokens, pairs * PAIR), bf16)] * 3,
        scratch_shapes=[
            pltpu.VMEM((2, tokens, PAIR), bf16),
            pltpu.VMEM((2, tokens, PAIR), bf16),
            pltpu.VMEM((PAIR, tokens), f32),
        ],
        compiler_params=pltpu.CompilerParams(
            dimension_semantics=("arbitrary", "arbitrary"), vmem_limit_bytes=58 * 2**20
        ),
        cost_estimate=pl.CostEstimate(
            flops=40 * pairs * tokens * tokens * PAIR,
            bytes_accessed=pairs * tokens * PAIR * 24,
            transcendentals=pairs * 2 * tokens * tokens,
        ),
    )(valid, proj, proj, proj, grad, attended, logs)


def exchange(values, axis):
    return lax.all_to_all(values, axis, split_axis=0, concat_axis=0, tiled=True)


def sum_everywhere(values):
    for axis in ("dp", "mp"):
        size = lax.axis_size(axis)
        bit = 1
        while bit < size:
            values = values + lax.ppermute(values, axis, [(i, i ^ bit) for i in range(size)])
            bit *= 2
    return values


def per_device(
    inputs,
    teacher,
    clip_tokens,
    owners,
    qkv_master,
    out_master,
    up_master,
    down_master,
    norm_gains,
    shift_vectors,
    split_vectors,
    bases,
    first_moments,
    second_moments,
    plain_first,
    plain_second,
    split_first,
    split_second,
):
    local_rows, clips_here, width = inputs.shape
    groups = lax.axis_size("mp")
    group_index = lax.axis_index("mp")
    shard_count = lax.axis_size("dp")
    shard_index = lax.axis_index("dp")
    seq_len = local_rows * groups
    row_blocks, shard_rows, _, group_width = qkv_master.shape
    group_ff = up_master.shape[2]
    ff = group_ff * groups
    tokens_here = clips_here * local_rows
    parts = groups // clips_here
    part_groups = groups // parts
    part_width = part_groups * group_width
    my_clip = group_index // parts
    my_part = group_index % parts
    pairs = part_width // PAIR
    calls = 2
    call_pairs = pairs // calls
    call_width = call_pairs * PAIR
    row_block = seq_len // 7

    positions = group_index * local_rows + jnp.arange(local_rows)
    row_valid = positions[None, :] < clip_tokens[:, None]
    valid = lax.dynamic_slice(clip_tokens, (my_clip,), (1,))

    split_all = lax.all_gather(split_vectors[0], "mp", axis=0)
    qkv_groups = lax.all_gather(
        qkv_master.astype(bf16).reshape(row_blocks, shard_rows, 3 * group_width), "mp", axis=0
    )
    qkv_part = lax.dynamic_slice_in_dim(qkv_groups, my_part * part_groups, part_groups, axis=0)
    qkv_part = (
        qkv_part.reshape(part_groups, row_blocks, shard_rows, 3, group_width)
        .transpose(1, 2, 3, 0, 4)
        .reshape(row_blocks, shard_rows, 3 * part_width)
    )
    qkv_weight = lax.all_gather(qkv_part, "dp", axis=1, tiled=True).reshape(width, 3 * part_width)

    def both_axes(master, mp_axis):
        over_mp = lax.all_gather(master.astype(bf16), "mp", axis=mp_axis, tiled=True)
        return lax.all_gather(over_mp, "dp", axis=1, tiled=True)

    out_weight = both_axes(out_master, 0).reshape(width, width)
    up_weight = both_axes(up_master, 2).reshape(width, ff)
    down_weight = both_axes(down_master, 0).reshape(ff, width)
    part_bias = lax.dynamic_slice_in_dim(
        split_all[:, : 2 * group_width].reshape(groups, 2, group_width),
        my_part * part_groups,
        part_groups,
        axis=0,
    ).transpose(1, 0, 2).reshape(2, part_width)
    up_bias = split_all[:, 2 * group_width :].reshape(ff)

    tokens = inputs.transpose(1, 0, 2).astype(f32)
    normed = layer_norm(tokens, norm_gains[0], shift_vectors[0]).astype(bf16)
    normed_clip = exchange(jnp.repeat(normed, parts, axis=0), "mp").reshape(seq_len, width)
    proj_bias = jnp.concatenate([part_bias[0], jnp.zeros_like(part_bias[0]), part_bias[1]])
    proj = (dot(normed_clip, qkv_weight) + proj_bias).astype(bf16)
    attended_parts, log_parts, received = [], [], []
    for call in range(calls):
        attended_call, logs_call = attend_forward(
            proj, valid, call * call_pairs, call_pairs, row_block
        )
        attended_parts.append(attended_call)
        log_parts.append(logs_call)
        received.append(exchange(attended_call.reshape(groups, local_rows, call_width), "mp"))
    attended = (
        jnp.stack(received)
        .reshape(calls, clips_here, parts, local_rows, call_width)
        .transpose(1, 3, 2, 0, 4)
        .reshape(tokens_here, width)
    )
    tokens = tokens.reshape(tokens_here, width)
    hidden = tokens + dot(attended, out_weight) + shift_vectors[1]
    normed_two = layer_norm(hidden, norm_gains[1], shift_vectors[2]).astype(bf16)
    upper = dot(normed_two, up_weight) + up_bias
    gelu = partial(jax.nn.gelu, approximate=False)
    active, gelu_pull = jax.vjp(gelu, upper)
    active = active.astype(bf16)
    final = hidden + dot(active, down_weight) + shift_vectors[3]
    output = final.astype(bf16).reshape(clips_here, local_rows, width).transpose(1, 0, 2)

    target = teacher.transpose(1, 0, 2).reshape(tokens_here, width).astype(f32)
    grad_final = jnp.where(row_valid.reshape(tokens_here, 1), final - target, 0.0)
    grad_final_low = grad_final.astype(bf16)
    grad_active = dot(grad_final_low, down_weight, NT)
    grad_upper = gelu_pull(grad_active)[0].astype(bf16)
    grad_normed_two = dot(grad_upper, up_weight, NT)
    _, norm_two_pull = jax.vjp(layer_norm, hidden, norm_gains[1], shift_vectors[2])
    hidden_part, grad_gain_two, grad_shift_two = norm_two_pull(grad_normed_two)
    grad_hidden = grad_final + hidden_part
    grad_hidden_low = grad_hidden.astype(bf16)
    grad_attended = dot(grad_hidden_low, out_weight, NT).astype(bf16)
    outgoing_grad = (
        grad_attended.reshape(clips_here, local_rows, parts, calls, call_width)
        .transpose(3, 0, 2, 1, 4)
        .reshape(calls, groups, local_rows, call_width)
    )
    grad_parts = [
        exchange(outgoing_grad[call], "mp").reshape(seq_len, call_width) for call in range(calls)
    ]

    def scatter_rows(grad, shape):
        return lax.psum_scatter(
            grad.astype(bf16).reshape(shape), "dp", scatter_dimension=1, tiled=True
        )

    grad_down = scatter_rows(dot(active, grad_final_low, TN), (ff // B, B, width))
    grad_up = scatter_rows(dot(normed_two, grad_upper, TN), (row_blocks, B, ff))
    grad_out = scatter_rows(dot(attended, grad_hidden_low, TN), (width // B, B, width))
    early = jnp.concatenate(
        [
            jnp.sum(grad_hidden, axis=0),
            grad_gain_two,
            grad_shift_two,
            jnp.sum(grad_final, axis=0),
            jnp.sum(grad_upper, axis=0, dtype=f32),
        ]
    )
    early_total = sum_everywhere(early.reshape(-1, width))
    by_group = jnp.concatenate(
        [
            grad_out.reshape(groups, -1, shard_rows, width),
            grad_up.reshape(row_blocks, shard_rows, groups, group_ff).transpose(2, 0, 1, 3),
            grad_down.reshape(groups, -1, shard_rows, width),
        ],
        axis=1,
    )
    own = jnp.sum(
        exchange(by_group, "mp").reshape(groups, -1, shard_rows, width).astype(f32), axis=0
    )
    count = group_width // B
    out_shard, up_shard, down_shard = own[:count], own[count : count + row_blocks], own[count + row_blocks :]

    pieces = []
    for call in range(calls):
        pieces.append(
            attend_backward(
                proj,
                grad_parts[call],
                attended_parts[call],
                log_parts[call],
                valid,
                call * call_pairs,
                call_pairs,
                row_block,
            )
        )
    grad_proj = jnp.concatenate([piece[kind] for kind in range(3) for piece in pieces], axis=1)
    grad_normed_part = dot(grad_proj, qkv_weight, NT).astype(bf16)
    grad_qkv = scatter_rows(
        dot(normed_clip, grad_proj, TN), (row_blocks, B, 3 * part_width)
    )
    returned_grad = exchange(grad_normed_part.reshape(groups, local_rows, width), "mp")
    grad_normed = jnp.sum(
        returned_grad.reshape(clips_here, parts, local_rows, width).astype(f32), axis=1
    ).reshape(tokens_here, width)
    _, norm_one_pull = jax.vjp(layer_norm, tokens, norm_gains[0], shift_vectors[0])
    tokens_part, grad_gain_one, grad_shift_one = norm_one_pull(grad_normed)
    input_grad = (
        (grad_hidden + tokens_part).reshape(clips_here, local_rows, width).transpose(1, 0, 2)
    )
    part_sums = jnp.sum(grad_proj, axis=0, dtype=f32).reshape(3, part_width)
    placed_sums = jnp.where(
        jnp.arange(parts)[:, None, None] == my_part, part_sums[None, ::2], 0.0
    )
    bias_rows = placed_sums.transpose(1, 0, 2).reshape(2, width)
    late = jnp.concatenate([grad_gain_one[None], grad_shift_one[None], bias_rows])
    late_total = sum_everywhere(late)
    plain_total = jnp.concatenate([late_total[:2], early_total[:4]])
    split_grad = jnp.concatenate(
        [
            late_total[2].reshape(groups, group_width),
            late_total[3].reshape(groups, group_width),
            early_total[4:].reshape(groups, group_ff),
        ],
        axis=1,
    )
    split_total = lax.dynamic_slice_in_dim(split_grad, group_index, 1, axis=0)

    qkv_groups_grad = (
        grad_qkv.reshape(row_blocks, shard_rows, 3, part_groups, group_width)
        .transpose(3, 0, 1, 2, 4)
        .reshape(1, part_groups, row_blocks, shard_rows, 3 * group_width)
    )
    here = jnp.arange(parts)[:, None, None, None, None] == my_part
    qkv_sent = jnp.where(here, qkv_groups_grad, jnp.zeros((), bf16)).reshape(
        groups, row_blocks, shard_rows, 3 * group_width
    )
    qkv_shard = jnp.sum(
        exchange(qkv_sent, "mp").astype(f32), axis=0
    ).reshape(row_blocks, shard_rows, 3, group_width)

    grad_blocks = jnp.concatenate(
        [
            qkv_shard.reshape(row_blocks, shard_rows, 3, group_width // B, B)
            .transpose(0, 2, 3, 1, 4)
            .reshape(-1, shard_rows, B),
            out_shard.reshape(group_width // B, shard_rows, row_blocks, B)
            .transpose(0, 2, 1, 3)
            .reshape(-1, shard_rows, B),
            up_shard.reshape(row_blocks, shard_rows, group_ff // B, B)
            .transpose(0, 2, 1, 3)
            .reshape(-1, shard_rows, B),
            down_shard.reshape(group_ff // B, shard_rows, row_blocks, B)
            .transpose(0, 2, 1, 3)
            .reshape(-1, shard_rows, B),
        ],
        axis=0,
    ).astype(bf16)
    cap_count = bases.shape[0]
    block_ids = jnp.arange(owners.shape[0])
    same_owner = owners[:, None] == owners[None, :]
    earlier = block_ids[None, :] < block_ids[:, None]
    slot_pos = jnp.sum((same_owner & earlier).astype(jnp.int32), axis=1)
    select = (
        (slot_pos[None, None, :] == jnp.arange(cap_count)[:, None, None])
        & (owners[None, None, :] == jnp.arange(shard_count)[None, :, None])
    ).astype(bf16)
    outgoing = jnp.einsum("cjk,krb->cjrb", select, grad_blocks, preferred_element_type=bf16)
    incoming = (
        lax.all_to_all(outgoing, "dp", split_axis=1, concat_axis=1, tiled=True)
        .astype(f32)
        .reshape(cap_count, B, B)
    )
    slot_used = jnp.any(
        (owners[None, :] == shard_index) & (slot_pos[None, :] == jnp.arange(cap_count)[:, None]),
        axis=1,
    )
    old_first = first_moments[:, 0]
    old_second = second_moments[:, 0]
    new_first, new_second, update = rotate_adam(
        incoming, bases[:, 0, 0], bases[:, 0, 1], old_first, old_second
    )
    first_new = jnp.where(slot_used[:, None, None], new_first, old_first)[:, None]
    second_new = jnp.where(slot_used[:, None, None], new_second, old_second)[:, None]
    returned = lax.all_to_all(
        update.reshape(cap_count, shard_count, shard_rows, B).astype(bf16),
        "dp",
        split_axis=1,
        concat_axis=1,
        tiled=True,
    )
    picked = jnp.take(
        returned.reshape(cap_count * shard_count, shard_rows, B),
        slot_pos * shard_count + owners,
        axis=0,
    ).astype(f32)
    count_qkv = row_blocks * 3 * (group_width // B)
    count_out = group_width // B * row_blocks
    count_up = row_blocks * (group_ff // B)
    qkv_update = (
        picked[:count_qkv]
        .reshape(row_blocks, 3, group_width // B, shard_rows, B)
        .transpose(0, 3, 1, 2, 4)
        .reshape(row_blocks, shard_rows, 3, group_width)
    )
    out_update = (
        picked[count_qkv : count_qkv + count_out]
        .reshape(group_width // B, row_blocks, shard_rows, B)
        .transpose(0, 2, 1, 3)
        .reshape(group_width // B, shard_rows, width)
    )
    up_update = (
        picked[count_qkv + count_out : count_qkv + count_out + count_up]
        .reshape(row_blocks, group_ff // B, shard_rows, B)
        .transpose(0, 2, 1, 3)
        .reshape(row_blocks, shard_rows, group_ff)
    )
    down_update = (
        picked[count_qkv + count_out + count_up :]
        .reshape(group_ff // B, row_blocks, shard_rows, B)
        .transpose(0, 2, 1, 3)
        .reshape(group_ff // B, shard_rows, width)
    )
    qkv_new = qkv_master - rate_qkv * qkv_update
    out_new = out_master - rate_out * out_update
    up_new = up_master - rate_up * up_update
    down_new = down_master - rate_down * down_update
    plain_param = jnp.stack(
        [
            norm_gains[0],
            shift_vectors[0],
            shift_vectors[1],
            norm_gains[1],
            shift_vectors[2],
            shift_vectors[3],
        ]
    )
    plain_new, plain_first_new, plain_second_new = adam_rows(
        plain_total, plain_param, plain_first, plain_second
    )
    gains_new = jnp.stack([plain_new[0], plain_new[3]])
    shifts_new = jnp.stack([plain_new[1], plain_new[2], plain_new[4], plain_new[5]])
    split_new, split_first_new, split_second_new = adam_rows(
        split_total, split_vectors, split_first, split_second
    )
    return (
        output,
        input_grad,
        qkv_new,
        out_new,
        up_new,
        down_new,
        qkv_new.astype(bf16),
        out_new.astype(bf16),
        up_new.astype(bf16),
        down_new.astype(bf16),
        gains_new,
        shifts_new,
        split_new,
        first_new,
        second_new,
        plain_first_new,
        plain_second_new,
        split_first_new,
        split_second_new,
    )


def solution(mesh):
    placed = (
        P("mp", "dp", None),
        P("mp", "dp", None),
        P("dp"),
        P(),
        P(None, "dp", None, "mp"),
        P("mp", "dp", None),
        P(None, "dp", "mp"),
        P("mp", "dp", None),
        P(),
        P(),
        P("mp", None),
        P("dp", "mp", None, None, None),
        P("dp", "mp", None, None),
        P("dp", "mp", None, None),
        P(),
        P(),
        P("mp", None),
        P("mp", None),
    )
    return jax.shard_map(
        per_device,
        mesh=mesh,
        in_specs=placed,
        out_specs=(
            P("mp", "dp", None),
            P("mp", "dp", None),
            P(None, "dp", None, "mp"),
            P("mp", "dp", None),
            P(None, "dp", "mp"),
            P("mp", "dp", None),
            P(None, "dp", None, "mp"),
            P("mp", "dp", None),
            P(None, "dp", "mp"),
            P("mp", "dp", None),
            P(),
            P(),
            P("mp", None),
            P("dp", "mp", None, None),
            P("dp", "mp", None, None),
            P(),
            P(),
            P("mp", None),
            P("mp", None),
        ),
        check_vma=False,
    )
```

time: 1610 us -> 883 us (0.55)
  waiting for transfers between devices: 884 us -> 273 us
  matrix products: 352 us -> 170 us
  other arithmetic: 196 us -> 50.9 us
  Pallas kernels: 0 us -> 101 us
  blocking collectives: 82.8 us -> 134 us
  starting transfers between devices: 9.08 us -> 55.5 us
    all_gather x7 -> x6, waiting for transfers between devices: 475 us -> 7.64 us  [the longest x3 7.6 us: both_axes(): return lax.all_gather(over_mp, 'dp', axis=1, tiled=True)]
    unnamed x19 -> x10, waiting for transfers between devices: 340 us -> 1 us
    dot_general x29 -> x17, matrix products: 352 us -> 170 us  [the longest x12 159 us: dot(): return lax.dot_general(left, right, dims, preferred_element_type=f32)]
    all_gather x1 -> x3, blocking collectives: 13.5 us -> 134 us  [the longest x1 89.5 us: per_device(): split_all = lax.all_gather(split_vectors[0], 'mp', axis=0)]
    convert_element_type x16 -> x12, other arithmetic: 118 us -> 11 us  [the longest x3 2.53 us: both_axes(): master.astype(bf16)]
    pallas_call x0 -> x4, Pallas kernels: none -> 101 us  [the longest x2 70.9 us: attend_backward(): pl.pallas_call(backward_kernel, grid=(pairs, tokens // row_block), in_spe...]
    all_to_all x1 -> x9, waiting for transfers between devices: 17.1 us -> 104 us  [the longest x8 94.6 us: exchange(): return lax.all_to_all(values, axis, split_axis=0, concat_axis=0, tiled=True)]
    psum x2 -> x0, blocking collectives: 69.3 us -> none  [the longest x1 40.9 us: per_device(): plain_total = lax.psum(plain_local, ('dp', 'mp'))]
  transfers between devices with their start and end apart: 17 -> 30, of which waited for: 13 -> 16; matrix products, arithmetic and copies ran while one was open for 25% -> 21% of each run, Pallas kernels for 0% -> 7%
where the time goes in v1:
time: 883 us; the launch traced here: 877 us
  waiting for transfers between devices  273 us (31%)
  matrix products  170 us (19%)
  blocking collectives  134 us (15%)
  Pallas kernels  101 us (11%)
  local copies, waits for them, and re-layouts  77 us (9%)
  starting transfers between devices  55.5 us (6%)
  other arithmetic  50.9 us (6%)
  between operations  16.2 us (2%)
    dot_general x12, matrix products, dot(): return lax.dot_general(left, right, dims, preferred_element_type=f32)  159 us
    reduce_scatter x4, waiting for transfers between devices, scatter_rows(): lax.psum_scatter(grad.astype(bf16).reshape(shape), 'dp', scatter_dimensio...  96.2 us
    all_to_all x8, waiting for transfers between devices, exchange(): return lax.all_to_all(values, axis, split_axis=0, concat_axis=0, tiled=True)  94.6 us
    all_gather x1, blocking collectives, per_device(): split_all = lax.all_gather(split_vectors[0], 'mp', axis=0)  89.5 us
    pallas_call x2, Pallas kernels, attend_backward(): pl.pallas_call(backward_kernel, grid=(pairs, tokens // row_block), in_spe...  70.9 us
    ppermute x10, waiting for transfers between devices, sum_everywhere(): lax.ppermute(values, axis, [(i, i ^ bit) for i in range(size)])  51.1 us
    all_to_all x8, starting transfers between devices, exchange(): return lax.all_to_all(values, axis, split_axis=0, concat_axis=0, tiled=True)  36 us
    pallas_call x2, Pallas kernels, attend_forward(): pl.pallas_call(partial(forward_kernel, chunk), grid=(pairs,), in_specs=[p...  30 us
  transfers between devices with their start and end apart: 30, of which 16 were waited for; matrix products, arithmetic and copies ran while one was open for 21% of the time, Pallas kernels for 7%

profile of v1, /device:TPU:0, one launch (start us, length us, event | category | flops | bytes accessed | tf_op | source)
XLA Modules:
  0.0 877.3 jit_solution(3097007169143158310)
XLA Ops:
  10.6 27.4 %all_gather.27 = bf16[4,8,16,768]{3,2,1,0:T(8,128)(2,1)S(1)} all-gather(bf16[1,8,16,768]{3,2,1,0:T(8,128)(2,1)S(1)} %all_gather_reshape.3), channel_id=1, replica_groups=mesh['dp'=8,'mp'=4] {'mp'}, dimensions={0}, use_global_device_ids=true | all-gather | bytes 983040 | tf_op jit(solution)/shard_map/all_gather | solution.py:332
  40.7 16.6 %all_gather.30 = bf16[8,16,1024]{2,1,0:T(8,128)(2,1)} all-gather(bf16[2,16,1024]{2,1,0:T(8,128)(2,1)S(1)} %convert_element_type.124), channel_id=1, replica_groups=mesh['dp'=8,'mp'=4] {'mp'}, dimensions={0}, use_global_device_ids=true | all-gather | bytes 327680 | tf_op jit(solution)/shard_map/all_gather | solution.py:344
  68.0 89.5 %all-gather = f32[4,1,1536]{2,1,0:T(1,128)S(1)} all-gather(f32[1,1,1536]{2,1,0:T(1,128)S(1)} %bitcast.323), channel_id=1, replica_groups=mesh['dp'=8,'mp'=4] {'mp'}, dimensions={0}, use_global_device_ids=true | all-gather | bytes 30720 | tf_op jit(solution)/shard_map/all_gather | solution.py:331
  158.3 9.2 %add_convert_fusion.1.q_ref.k_ref.v_ref = bf16[1568,1536]{1,0:T(8,128)(2,1)} fusion(bf16[1568,1024]{1,0:T(8,128)(2,1)} %bitcast.5, bf16[1024,1536]{1,0:T(8,128)(2,1)} %bitcast.336, f32[1536]{0:T(1024)S(1)} %pad_maximum_fusion.4), kind=kOutput, calls=%fused_computation.20 | convolution fusion | flops 4937318400 | bytes 11180032 | tf_op jit(solution)/shard_map/dot_general | solution.py:34
  167.4 15.0 %shard_map.321 = (bf16[1568,256]{1,0:T(8,128)(2,1)}, f32[1568,256]{1,0:T(8,128)}) custom-call(s32[1]{0:T(128)} %dynamic_slice.12.valid_ref, bf16[1568,1536]{1,0:T(8,128)(2,1)} %add_convert_fusion.1.q_ref.k_ref.v_ref, bf16[1568,1536]{1,0:T(8,128)(2,1)} %add_convert_fusion.1.q_ref.k_ref.v_ref, bf16[1568,1536]{1,0:T(8,128)(2,1)} %add_convert_fusion.1.q_ref.k_ref.v_ref), custom_call_target="tpu_custom_call" | custom-call | flops 10070523904 | bytes 4816896 | tf_op jit(solution)/shard_map/pallas_call | solution.py:130
  188.1 15.0 %shard_map.322 = (bf16[1568,256]{1,0:T(8,128)(2,1)}, f32[1568,256]{1,0:T(8,128)}) custom-call(s32[1]{0:T(128)} %dynamic_slice.12.valid_ref, bf16[1568,1536]{1,0:T(8,128)(2,1)} %add_convert_fusion.1.q_ref.k_ref.v_ref, bf16[1568,1536]{1,0:T(8,128)(2,1)} %add_convert_fusion.1.q_ref.k_ref.v_ref, bf16[1568,1536]{1,0:T(8,128)(2,1)} %add_convert_fusion.1.q_ref.k_ref.v_ref), custom_call_target="tpu_custom_call" | custom-call | flops 10070523904 | bytes 4816896 | tf_op jit(solution)/shard_map/pallas_call | solution.py:130
  213.9 12.7 %all-to-all-done.2 = bf16[4,392,256]{2,1,0:T(8,128)(2,1)S(1)} async-done(((bf16[4,392,256]{2,1,0:T(8,128)(2,1)}), bf16[4,392,256]{2,1,0:T(8,128)(2,1)S(1)}, u32[]{:S(2)}, u32[]{:S(2)}) %all-to-all-start.2) | async-done | bytes 802848 | tf_op jit(solution)/shard_map/all_to_all | solution.py:273
  236.8 39.9 %multiply_convert_fusion = (bf16[784,4096]{1,0:T(8,128)(2,1)}, f32[784,4096]{1,0:T(8,128)}, f32[784,4096]{1,0:T(8,128)}) fusion(f32[4096]{0:T(1024)S(1)} %bitcast.325, bf16[1024,4096]{1,0:T(8,128)(2,1)} %bitcast.332, f32[784,1024]{1,0:T(8,128)S(1)} %bitcast_add_fusion, f32[1024]{0:T(1024)S(1)} %bitcast.329, f32[1024]{0:T(1024)S(1)} %bitcast.318, ...), kind=kOutput, calls=%fused_computation.5 | convolution fusion | flops 6793428992 | bytes 43747456 | tf_op jit(solution)/shard_map/dot_general | solution.py:34
  284.3 14.1 %fusion.89 = (f32[1024]{0:T(1024)}, f32[784,1024]{1,0:T(8,128)}, bf16[784,1024]{1,0:T(8,128)(2,1)}) fusion(f32[2,392,1024]{2,1,0:T(8,128)} %copy.279, pred[784]{0:T(1024)(128)(4,1)S(1)} %lt.61, f32[1024]{0:T(1024)S(1)} %bitcast.331, bf16[784,4096]{1,0:T(8,128)(2,1)} %get-tuple-element.222, bf16[4096,1024]{1,0:T(8,128)(2,1)} %bitcast.334, ...), kind=kOutput, calls=%fused_computation.206 | convolution fusion | flops 6582287360 | bytes 26063632 | tf_op jit(solution)/shard_map/dot_general | solution.py:34
  298.4 21.4 %convert_reduce_fusion = (f32[4096]{0:T(1024)S(1)}, bf16[784,4096]{1,0:T(8,128)(2,1)}) fusion(f32[784,4096]{1,0:T(8,128)} %get-tuple-element.223, bf16[4096,1024]{1,0:T(8,128)(2,1)} %bitcast.335, f32[784,1024]{1,0:T(8,128)} %get-tuple-element.207, f32[784,4096]{1,0:T(8,128)} %get-tuple-element.256, f32[4096]{0:T(1024)S(1)} %bitcast.326), kind=kOutput, calls=%fused_computation.3 | convolution fusion | flops 6632058880 | bytes 43745280 | tf_op jit(solution)/shard_map/dot_general | solution.py:34
  319.8 12.2 %multiply_reduce_fusion = (f32[1024]{0:T(1024)S(1)}, f32[784]{0:T(1024)S(1)}, f32[1024]{0:T(1024)S(1)}, f32[784,1024]{1,0:T(8,128)S(1)}) fusion(f32[784,1024]{1,0:T(8,128)S(1)} %bitcast_add_fusion, f32[784]{0:T(1024)S(1)} %fusion.77, f32[784]{0:T(1024)S(1)} %broadcast_multiply_fusion, f32[1024]{0:T(1024)S(1)} %bitcast.311, f32[1024]{0:T(1024)S(1)} %bitcast.319, ...), kind=kOutput, calls=%fused_computation.56 | convolution fusion | flops 6583890944 | bytes 21259456 | tf_op jit(solution)/shard_map/dot_general | solution.py:34
  357.8 18.5 %all-to-all-done.3 = bf16[4,392,256]{2,1,0:T(8,128)(2,1)} async-done(((bf16[4,392,256]{2,1,0:T(8,128)(2,1)}), bf16[4,392,256]{2,1,0:T(8,128)(2,1)}, u32[]{:S(2)}, u32[]{:S(2)}) %all-to-all-start.3) | async-done | bytes 802848 | tf_op jit(solution)/shard_map/all_to_all | solution.py:273
  380.6 35.3 %shard_map.323 = (bf16[1568,256]{1,0:T(8,128)(2,1)}, bf16[1568,256]{1,0:T(8,128)(2,1)}, bf16[1568,256]{1,0:T(8,128)(2,1)}) custom-call(s32[1]{0:T(128)} %dynamic_slice.12.valid_ref, bf16[1568,1536]{1,0:T(8,128)(2,1)} %add_convert_fusion.1.q_ref.k_ref.v_ref, bf16[1568,1536]{1,0:T(8,128)(2,1)} %add_convert_fusion.1.q_ref.k_ref.v_ref, ...), custom_call_target="tpu_custom_call" | custom-call | flops 25176309760 | bytes 9633792 | tf_op jit(solution)/shard_map/pallas_call | solution.py:242
  418.1 35.6 %shard_map.324 = (bf16[1568,256]{1,0:T(8,128)(2,1)}, bf16[1568,256]{1,0:T(8,128)(2,1)}, bf16[1568,256]{1,0:T(8,128)(2,1)}) custom-call(s32[1]{0:T(128)} %dynamic_slice.12.valid_ref, bf16[1568,1536]{1,0:T(8,128)(2,1)} %add_convert_fusion.1.q_ref.k_ref.v_ref, bf16[1568,1536]{1,0:T(8,128)(2,1)} %add_convert_fusion.1.q_ref.k_ref.v_ref, ...), custom_call_target="tpu_custom_call" | custom-call | flops 25176309760 | bytes 9633792 | tf_op jit(solution)/shard_map/pallas_call | solution.py:242
  460.0 10.1 %convolution_convert_fusion.2 = bf16[1024,1536]{1,0:T(8,128)(2,1)} fusion(bf16[1568,1024]{1,0:T(8,128)(2,1)} %bitcast.5, bf16[1568,1536]{1,0:T(8,128)(2,1)} %constant_dynamic-update-slice_fusion), kind=kOutput, calls=%fused_computation.28 | convolution fusion | flops 4934074368 | bytes 11173888 | tf_op jit(solution)/shard_map/dot_general | solution.py:34
  476.8 15.2 %convolution_convert_fusion.1 = bf16[4096,1024]{1,0:T(8,128)(2,1)} fusion(bf16[784,4096]{1,0:T(8,128)(2,1)} %get-tuple-element.222, f32[784,1024]{1,0:T(8,128)} %get-tuple-element.207), kind=kOutput, calls=%fused_computation.22 | convolution fusion | flops 6581665792 | bytes 18022400 | tf_op jit(solution)/shard_map/dot_general | solution.py:34
  492.7 14.4 %convolution_convert_fusion = bf16[1024,4096]{1,0:T(8,128)(2,1)} fusion(bf16[784,4096]{1,0:T(8,128)(2,1)} %get-tuple-element.260, f32[784,1024]{1,0:T(8,128)S(1)} %bitcast_add_fusion, f32[1024]{0:T(1024)S(1)} %bitcast.330, f32[1024]{0:T(1024)S(1)} %bitcast.321, f32[784]{0:T(1024)S(1)} %fusion.77, f32[784]{0:T(1024)S(1)} %broadcast_multiply_fusion, ...), kind=kOutput, calls=%fused_computation.21 | convolution fusion | flops 6585679872 | bytes 18040960 | tf_op jit(solution)/shard_map/dot_general | solution.py:34
  509.0 9.0 %convolution_convert_fusion.3 = bf16[1568,1024]{1,0:T(8,128)(2,1)} fusion(bf16[1568,1536]{1,0:T(8,128)(2,1)} %constant_dynamic-update-slice_fusion, bf16[1024,1536]{1,0:T(8,128)(2,1)S(1)} %bitcast.337), kind=kOutput, calls=%fused_computation.29 | convolution fusion | flops 4934107136 | bytes 11173888 | tf_op jit(solution)/shard_map/dot_general | solution.py:34
  532.5 62.2 %all-to-all-done.5 = bf16[4,392,1024]{2,1,0:T(8,128)(2,1)S(1)} async-done(((bf16[4,392,1024]{2,1,0:T(8,128)(2,1)}), bf16[4,392,1024]{2,1,0:T(8,128)(2,1)S(1)}, u32[]{:S(2)}, u32[]{:S(2)}) %all-to-all-start.5) | async-done | bytes 3211296 | tf_op jit(solution)/shard_map/all_to_all | solution.py:273
  612.9 24.4 %reduce-scatter.11.cloned.1.call-done = bf16[32,16,1024]{2,1,0:T(8,128)(2,1)} async-done(((bf16[32,128,1024]{2,1,0:T(8,128)(2,1)}), bf16[32,16,1024]{2,1,0:T(8,128)(2,1)}) %reduce-scatter.11.cloned.1.call-update) | async-done | bytes 1048592 | tf_op jit(solution)/shard_map/reduce_scatter | solution.py:408
  640.4 71.7 %reduce-scatter.9.cloned.1.call-done = bf16[8,16,4096]{2,1,0:T(8,128)(2,1)} async-done(((bf16[8,128,4096]{2,1,0:T(8,128)(2,1)}), bf16[8,16,4096]{2,1,0:T(8,128)(2,1)}) %reduce-scatter.9.cloned.1.call-update) | async-done | bytes 1048592 | tf_op jit(solution)/shard_map/reduce_scatter | solution.py:408
  742.9 37.0 %collective-permute-done.9 = f32[8,1024]{1,0:T(8,128)S(1)} collective-permute-done((f32[8,1024]{1,0:T(8,128)S(1)}, f32[8,1024]{1,0:T(8,128)S(1)}, u32[]{:S(2)}, u32[]{:S(2)}) %collective-permute-start.9) | collective-permute-done | bytes 32800 | tf_op jit(solution)/shard_map/ppermute | solution.py:281
  811.9 9.8 %all-to-all-done.8 = bf16[48,8,16,128]{3,2,0,1:T(8,128)(2,1)S(1)} async-done(((bf16[48,8,16,128]{3,2,0,1:T(8,128)(2,1)}), bf16[48,8,16,128]{3,2,0,1:T(8,128)(2,1)S(1)}, u32[]{:S(2)}, u32[]{:S(2)}) %all-to-all-start.8) | async-done | bytes 1572896 | tf_op jit(solution)/shard_map/all_to_all | solution.py:526
  851.0 12.7 %all-to-all-done.9 = bf16[48,8,16,128]{3,2,0,1:T(8,128)(2,1)} async-done(((bf16[48,8,16,128]{3,2,0,1:T(8,128)(2,1)}), bf16[48,8,16,128]{3,2,0,1:T(8,128)(2,1)}, u32[]{:S(2)}, u32[]{:S(2)}) %all-to-all-start.9) | async-done | bytes 1572896 | tf_op jit(solution)/shard_map/all_to_all | solution.py:541
  (337 shorter events, 232.2 us)
Async XLA Ops:
  7.2 50.2 %all-gather.12.cloned.1.call-start = ((), (), s32[]{:S(2)}) async-start(), calls=%async_computation.16 | async-start | bytes 1310720 | tf_op jit(solution)/shard_map/all_gather | solution.py:344
  9.1 149.2 %all-gather.8.cloned.1.call-start = ((), (), s32[]{:S(2)}) async-start(), calls=%async_computation.14 | async-start | bytes 3538944 | tf_op jit(solution)/shard_map/all_gather | solution.py:341
  39.8 168.6 %all-gather.16.cloned.1.call-start = ((), (), s32[]{:S(2)}) async-start(), calls=%async_computation.18 | async-start | bytes 1310720 | tf_op jit(solution)/shard_map/all_gather | solution.py:344
  40.6 190.3 %all-gather.10.cloned.1.call-start = ((), (), s32[]{:S(2)}) async-start(), calls=%async_computation.15 | async-start | bytes 2359296 | tf_op jit(solution)/shard_map/all_gather | solution.py:345
  57.3 179.5 %all-gather.14.cloned.1.call-start = ((), (), s32[]{:S(2)}) async-start(), calls=%async_computation.17 | async-start | bytes 9437184 | tf_op jit(solution)/shard_map/all_gather | solution.py:345
  63.2 95.0 %all-to-all-start = ((bf16[4,392,1024]{2,1,0:T(8,128)(2,1)}), bf16[4,392,1024]{2,1,0:T(8,128)(2,1)}, u32[]{:S(2)}, u32[]{:S(2)}) async-start(bf16[4,392,1024]{2,1,0:T(8,128)(2,1)} %bitcast.267), calls=%async_computation | async-start | bytes 6422528 | tf_op jit(solution)/shard_map/all_to_all | solution.py:273
  182.4 21.8 %all-to-all-start.1 = ((bf16[4,392,256]{2,1,0:T(8,128)(2,1)}), bf16[4,392,256]{2,1,0:T(8,128)(2,1)S(1)}, u32[]{:S(2)}, u32[]{:S(2)}) async-start(bf16[4,392,256]{2,1,0:T(8,128)(2,1)} %bitcast.295), calls=%async_computation.1 | async-start | bytes 1605632 | tf_op jit(solution)/shard_map/all_to_all | solution.py:273
  204.2 22.5 %all-to-all-start.2 = ((bf16[4,392,256]{2,1,0:T(8,128)(2,1)}), bf16[4,392,256]{2,1,0:T(8,128)(2,1)S(1)}, u32[]{:S(2)}, u32[]{:S(2)}) async-start(bf16[4,392,256]{2,1,0:T(8,128)(2,1)} %bitcast.294), calls=%async_computation.2 | async-start | bytes 1605632 | tf_op jit(solution)/shard_map/all_to_all | solution.py:273
  208.2 76.1 %all-gather.18.cloned.1.call-start = ((), (), s32[]{:S(2)}) async-start(), calls=%async_computation.19 | async-start | bytes 9437184 | tf_op jit(solution)/shard_map/all_gather | solution.py:345
  350.8 25.6 %all-to-all-start.3 = ((bf16[4,392,256]{2,1,0:T(8,128)(2,1)}), bf16[4,392,256]{2,1,0:T(8,128)(2,1)}, u32[]{:S(2)}, u32[]{:S(2)}) async-start(bf16[4,392,256]{2,1,0:T(8,128)(2,1)} %bitcast.279), calls=%async_computation.3 | async-start | bytes 1605632 | tf_op jit(solution)/shard_map/all_to_all | solution.py:273
  376.3 41.7 %all-to-all-start.4 = ((bf16[4,392,256]{2,1,0:T(8,128)(2,1)}), bf16[4,392,256]{2,1,0:T(8,128)(2,1)}, u32[]{:S(2)}, u32[]{:S(2)}) async-start(bf16[4,392,256]{2,1,0:T(8,128)(2,1)} %bitcast.278), calls=%async_computation.4 | async-start | bytes 1605632 | tf_op jit(solution)/shard_map/all_to_all | solution.py:273
  380.6 143.9 %reduce-scatter.5.cloned.1.call-start = ((), (), s32[]{:S(2)}) async-start(), calls=%async_computation.20 | async-start | bytes 3538944 | tf_op jit(solution)/shard_map/reduce_scatter | solution.py:408
  470.2 141.6 %reduce-scatter.7.cloned.1.call-start = ((), (), s32[]{:S(2)}) async-start(), calls=%async_computation.21 | async-start | bytes 2359296 | tf_op jit(solution)/shard_map/reduce_scatter | solution.py:408
  476.7 160.6 %reduce-scatter.11.cloned.1.call-start = ((), (), s32[]{:S(2)}) async-start(), calls=%async_computation.23 | async-start | bytes 9437184 | tf_op jit(solution)/shard_map/reduce_scatter | solution.py:408
  492.1 220.0 %reduce-scatter.9.cloned.1.call-start = ((), (), s32[]{:S(2)}) async-start(), calls=%async_computation.22 | async-start | bytes 9437184 | tf_op jit(solution)/shard_map/reduce_scatter | solution.py:408
  518.0 76.7 %all-to-all-start.5 = ((bf16[4,392,1024]{2,1,0:T(8,128)(2,1)}), bf16[4,392,1024]{2,1,0:T(8,128)(2,1)S(1)}, u32[]{:S(2)}, u32[]{:S(2)}) async-start(bf16[4,392,1024]{2,1,0:T(8,128)(2,1)} %bitcast.275), calls=%async_computation.5 | async-start | bytes 6422528 | tf_op jit(solution)/shard_map/all_to_all | solution.py:273
  594.7 125.0 %all-to-all-start.6 = ((bf16[4,8,16,768]{3,2,1,0:T(8,128)(2,1)}), bf16[4,8,16,768]{3,2,1,0:T(8,128)(2,1)}, u32[]{:S(2)}, u32[]{:S(2)}) async-start(bf16[4,8,16,768]{3,2,1,0:T(8,128)(2,1)} %bitcast_select_fusion.2), calls=%async_computation.7 | async-start | bytes 1572864 | tf_op jit(solution)/shard_map/all_to_all | solution.py:273
  609.8 115.0 %collective-permute-start.8 = (f32[8,1024]{1,0:T(8,128)S(1)}, f32[8,1024]{1,0:T(8,128)S(1)}, u32[]{:S(2)}, u32[]{:S(2)}) collective-permute-start(f32[8,1024]{1,0:T(8,128)S(1)} %add.287), channel_id=1, source_target_pairs={{0,1},{1,0},{2,3},{3,2},{4,5},{5,4},{6,7},{7,6},{8,9},{9,8},{10,11... | collective-permute-start | bytes 98312 | tf_op jit(solution)/shard_map/ppermute | solution.py:281
  719.7 73.0 %all-to-all-start.7 = ((bf16[4,18,16,1024]{3,2,1,0:T(8,128)(2,1)}), bf16[4,18,16,1024]{3,2,1,0:T(8,128)(2,1)}, u32[]{:S(2)}, u32[]{:S(2)}) async-start(bf16[4,18,16,1024]{3,2,1,0:T(8,128)(2,1)} %copy.292), calls=%async_computation.11 | async-start | bytes 4718592 | tf_op jit(solution)/shard_map/all_to_all | solution.py:273
  724.8 55.1 %collective-permute-start.9 = (f32[8,1024]{1,0:T(8,128)S(1)}, f32[8,1024]{1,0:T(8,128)S(1)}, u32[]{:S(2)}, u32[]{:S(2)}) collective-permute-start(f32[8,1024]{1,0:T(8,128)S(1)} %add.288), channel_id=1, source_target_pairs={{0,2},{1,3},{2,0},{3,1},{4,6},{5,7},{6,4},{7,5},{8,10},{9,11},{10,... | collective-permute-start | bytes 98312 | tf_op jit(solution)/shard_map/ppermute | solution.py:281
  739.8 40.0 %collective-permute-start = (f32[4,1024]{1,0:T(4,128)S(1)}, f32[4,1024]{1,0:T(4,128)S(1)}, u32[]{:S(2)}, u32[]{:S(2)}) collective-permute-start(f32[4,1024]{1,0:T(4,128)S(1)} %pad_maximum_fusion.2), channel_id=1, source_target_pairs={{0,4},{4,0},{8,12},{12,8},{16,20},{20,16},{24,28},{28,24},{1,5},{5... | collective-permute-start | bytes 49160 | tf_op jit(solution)/shard_map/ppermute | solution.py:281
  791.2 17.9 %collective-permute-start.4 = (f32[4,1024]{1,0:T(4,128)S(1)}, f32[4,1024]{1,0:T(4,128)S(1)}, u32[]{:S(2)}, u32[]{:S(2)}) collective-permute-start(f32[4,1024]{1,0:T(4,128)S(1)} %add.283), channel_id=1, source_target_pairs={{0,2},{1,3},{2,0},{3,1},{4,6},{5,7},{6,4},{7,5},{8,10},{9,11},{10,... | collective-permute-start | bytes 49160 | tf_op jit(solution)/shard_map/ppermute | solution.py:281
  797.2 24.5 %all-to-all-start.8 = ((bf16[48,8,16,128]{3,2,0,1:T(8,128)(2,1)}), bf16[48,8,16,128]{3,2,0,1:T(8,128)(2,1)S(1)}, u32[]{:S(2)}, u32[]{:S(2)}) async-start(bf16[48,8,16,128]{3,2,0,1:T(8,128)(2,1)} %copy.297), calls=%async_computation.12 | async-start | bytes 3145728 | tf_op jit(solution)/shard_map/all_to_all | solution.py:526
  838.3 25.3 %all-to-all-start.9 = ((bf16[48,8,16,128]{3,2,0,1:T(8,128)(2,1)}), bf16[48,8,16,128]{3,2,0,1:T(8,128)(2,1)}, u32[]{:S(2)}, u32[]{:S(2)}) async-start(bf16[48,8,16,128]{3,2,0,1:T(8,128)(2,1)} %copy.305), calls=%async_computation.13 | async-start | bytes 3145728 | tf_op jit(solution)/shard_map/all_to_all | solution.py:541
  (62 other events, 889.6 us)
Sparse Core Ops, SparseCore 0:
  10.1 37.9 all-gather.11
  50.6 32.8 all-gather.7
  85.7 52.8 all-gather.15
  140.4 31.7 all-gather.9
  173.9 54.2 all-gather.13
  230.0 54.2 all-gather.17
  470.3 46.4 reduce-scatter.4
  520.6 41.0 reduce-scatter.6
  565.2 72.0 reduce-scatter.10
  640.7 71.3 reduce-scatter.8

commit v2 on v1

--- a/solution.py
+++ b/solution.py
@@ -6,6 +6,7 @@
 from jax.experimental import pallas as pl
 from jax.experimental.pallas import tpu as pltpu
 from jax.sharding import PartitionSpec as P
+
 
 HD = 64
 B = 128
@@ -269,8 +270,74 @@
     )(valid, proj, proj, proj, grad, attended, logs)
 
 
+def feed_kernel(chunk, normed_ref, weight_ref, bias_ref, active_ref, slope_ref):
+    for at in range(0, normed_ref.shape[0], chunk):
+        rows = slice(at, at + chunk)
+        upper = dot(normed_ref[rows], weight_ref[...]) + bias_ref[...]
+        below = 0.5 + 0.5 * lax.erf(upper * 0.7071067811865476)
+        active_ref[rows] = (upper * below).astype(bf16)
+        density = 0.3989422804014327 * jnp.exp(-0.5 * upper * upper)
+        slope_ref[rows] = (below + upper * density).astype(bf16)
+
+
+def feed_up(normed, weight, bias):
+    tokens, width = normed.shape
+    columns = 512
+    by_column = pl.BlockSpec((tokens, columns), lambda step: (0, step))
+    return pl.pallas_call(
+        partial(feed_kernel, tokens // 7),
+        grid=(weight.shape[1] // columns,),
+        in_specs=[
+            pl.BlockSpec((tokens, width), lambda step: (0, 0)),
+            pl.BlockSpec((width, columns), lambda step: (0, step)),
+            pl.BlockSpec((1, columns), lambda step: (0, step)),
+        ],
+        out_specs=[by_column, by_column],
+        out_shape=[jax.ShapeDtypeStruct((tokens, weight.shape[1]), bf16)] * 2,
+        compiler_params=pltpu.CompilerParams(
+            dimension_semantics=("arbitrary",), vmem_limit_bytes=48 * 2**20
+        ),
+        cost_estimate=pl.CostEstimate(
+            flops=2 * tokens * width * weight.shape[1],
+            bytes_accessed=4 * tokens * weight.shape[1] + 2 * width * weight.shape[1],
+            transcendentals=2 * tokens * weight.shape[1],
+        ),
+    )(normed, weight, bias)
+
+
 def exchange(values, axis):
     return lax.all_to_all(values, axis, split_axis=0, concat_axis=0, tiled=True)
+
+
+def gather(values, axis, dimension):
+    return lax.all_gather(values, axis, axis=dimension, tiled=True)
+
+
+def scatter(values):
+    return lax.psum_scatter(values, "dp", scatter_dimension=1, tiled=True)
+
+
+def send_steps(pieces, axis):
+    size = lax.axis_size(axis)
+    arrived = [pieces[0]]
+    for step in range(1, size):
+        arrived.append(lax.ppermute(pieces[step], axis, [(i, i ^ step) for i in range(size)]))
+    return arrived
+
+
+def send_all(values, axis):
+    size = lax.axis_size(axis)
+    arrived = [values]
+    for step in range(1, size):
+        arrived.append(lax.ppermute(values, axis, [(i, i ^ step) for i in range(size)]))
+    return jnp.concatenate(arrived, axis=0)
+
+
+def sum_pieces(pieces, axis):
+    total = None
+    for piece in send_steps(pieces, axis):
+        total = piece.astype(f32) if total is None else total + piece.astype(f32)
+    return total
 
 
 def sum_everywhere(values):
@@ -278,7 +345,8 @@
         size = lax.axis_size(axis)
         bit = 1
         while bit < size:
-            values = values + lax.ppermute(values, axis, [(i, i ^ bit) for i in range(size)])
+            other = lax.ppermute(values, axis, [(i, i ^ bit) for i in range(size)])
+            values = values + other
             bit *= 2
     return values
 
@@ -313,6 +381,7 @@
     group_ff = up_master.shape[2]
     ff = group_ff * groups
     tokens_here = clips_here * local_rows
+    assert groups == 4 and clips_here == 2
     parts = groups // clips_here
     part_groups = groups // parts
     part_width = part_groups * group_width
@@ -327,33 +396,50 @@
     positions = group_index * local_rows + jnp.arange(local_rows)
     row_valid = positions[None, :] < clip_tokens[:, None]
     valid = lax.dynamic_slice(clip_tokens, (my_clip,), (1,))
-
-    split_all = lax.all_gather(split_vectors[0], "mp", axis=0)
-    qkv_groups = lax.all_gather(
-        qkv_master.astype(bf16).reshape(row_blocks, shard_rows, 3 * group_width), "mp", axis=0
-    )
-    qkv_part = lax.dynamic_slice_in_dim(qkv_groups, my_part * part_groups, part_groups, axis=0)
+    near_order = group_index ^ jnp.arange(groups)
+
+    def near_first(pieces):
+        return [
+            lax.dynamic_index_in_dim(pieces, group_index ^ step, 0, keepdims=False)
+            for step in range(groups)
+        ]
+
+    near_picks = (near_order[:, None] == jnp.arange(groups)[None, :])[:, :, None]
+
+    split_near = send_all(split_vectors, "mp")
+    split_all = jnp.sum(jnp.where(near_picks, split_near[None], 0.0), axis=1)
+    count = group_width // B
+    qkv_rows = qkv_master.astype(bf16).reshape(row_blocks, shard_rows, 3 * group_width)
+    near = lax.ppermute(qkv_rows, "mp", [(1, 0), (3, 1), (0, 2), (2, 3)])
+    inner = lax.ppermute(qkv_rows, "mp", [(1, 2), (2, 1)])
+    outer = (group_index == 0) | (group_index == groups - 1)
+    inner = jnp.where(outer, qkv_rows, inner)
+    low_half = group_index < clips_here
+    qkv_part = jnp.stack(
+        [jnp.where(low_half, inner, near), jnp.where(low_half, near, inner)], axis=2
+    )
     qkv_part = (
-        qkv_part.reshape(part_groups, row_blocks, shard_rows, 3, group_width)
-        .transpose(1, 2, 3, 0, 4)
+        qkv_part.reshape(row_blocks, shard_rows, part_groups, 3, group_width)
+        .transpose(0, 1, 3, 2, 4)
         .reshape(row_blocks, shard_rows, 3 * part_width)
     )
-    qkv_weight = lax.all_gather(qkv_part, "dp", axis=1, tiled=True).reshape(width, 3 * part_width)
-
-    def both_axes(master, mp_axis):
-        over_mp = lax.all_gather(master.astype(bf16), "mp", axis=mp_axis, tiled=True)
-        return lax.all_gather(over_mp, "dp", axis=1, tiled=True)
-
-    out_weight = both_axes(out_master, 0).reshape(width, width)
-    up_weight = both_axes(up_master, 2).reshape(width, ff)
-    down_weight = both_axes(down_master, 0).reshape(ff, width)
+    out_up = jnp.concatenate([out_master.astype(bf16), up_master.astype(bf16)], axis=0)
+    out_up = send_all(out_up[None], "mp")
+    down_rows = send_all(down_master.astype(bf16), "mp")
+    out_rows = out_up[:, :count]
+    out_rows = jnp.stack(near_first(out_rows)).reshape(-1, shard_rows, width)
+    up_rows = out_up[:, count:].transpose(1, 2, 0, 3).reshape(row_blocks, shard_rows, ff)
+    qkv_weight = gather(qkv_part, "dp", 1).reshape(width, 3 * part_width)
+    out_weight = gather(out_rows, "dp", 1).reshape(width, width)
+    up_weight = gather(up_rows, "dp", 1).reshape(width, ff)
+    down_weight = gather(down_rows, "dp", 1).reshape(ff, width)
     part_bias = lax.dynamic_slice_in_dim(
         split_all[:, : 2 * group_width].reshape(groups, 2, group_width),
         my_part * part_groups,
         part_groups,
         axis=0,
     ).transpose(1, 0, 2).reshape(2, part_width)
-    up_bias = split_all[:, 2 * group_width :].reshape(ff)
+    up_bias = split_near[:, 2 * group_width :].reshape(ff)
 
     tokens = inputs.transpose(1, 0, 2).astype(f32)
     normed = layer_norm(tokens, norm_gains[0], shift_vectors[0]).astype(bf16)
@@ -368,73 +454,75 @@
         attended_parts.append(attended_call)
         log_parts.append(logs_call)
         received.append(exchange(attended_call.reshape(groups, local_rows, call_width), "mp"))
-    attended = (
-        jnp.stack(received)
-        .reshape(calls, clips_here, parts, local_rows, call_width)
-        .transpose(1, 3, 2, 0, 4)
-        .reshape(tokens_here, width)
-    )
+    attended = jnp.stack(
+        [
+            jnp.concatenate(
+                [
+                    received[call][clip * parts + part]
+                    for part in range(parts)
+                    for call in range(calls)
+                ],
+                axis=1,
+            )
+            for clip in range(clips_here)
+        ]
+    ).reshape(tokens_here, width)
     tokens = tokens.reshape(tokens_here, width)
     hidden = tokens + dot(attended, out_weight) + shift_vectors[1]
     normed_two = layer_norm(hidden, norm_gains[1], shift_vectors[2]).astype(bf16)
-    upper = dot(normed_two, up_weight) + up_bias
-    gelu = partial(jax.nn.gelu, approximate=False)
-    active, gelu_pull = jax.vjp(gelu, upper)
-    active = active.astype(bf16)
+    active, slope = feed_up(normed_two, up_weight, up_bias.reshape(1, ff))
     final = hidden + dot(active, down_weight) + shift_vectors[3]
     output = final.astype(bf16).reshape(clips_here, local_rows, width).transpose(1, 0, 2)
 
     target = teacher.transpose(1, 0, 2).reshape(tokens_here, width).astype(f32)
     grad_final = jnp.where(row_valid.reshape(tokens_here, 1), final - target, 0.0)
     grad_final_low = grad_final.astype(bf16)
+    grad_down = dot(active, grad_final_low, TN).astype(bf16)
+    grad_final_low, grad_down = lax.optimization_barrier((grad_final_low, grad_down))
     grad_active = dot(grad_final_low, down_weight, NT)
-    grad_upper = gelu_pull(grad_active)[0].astype(bf16)
+    grad_upper = (grad_active * slope).astype(bf16)
     grad_normed_two = dot(grad_upper, up_weight, NT)
     _, norm_two_pull = jax.vjp(layer_norm, hidden, norm_gains[1], shift_vectors[2])
     hidden_part, grad_gain_two, grad_shift_two = norm_two_pull(grad_normed_two)
     grad_hidden = grad_final + hidden_part
     grad_hidden_low = grad_hidden.astype(bf16)
     grad_attended = dot(grad_hidden_low, out_weight, NT).astype(bf16)
-    outgoing_grad = (
-        grad_attended.reshape(clips_here, local_rows, parts, calls, call_width)
-        .transpose(3, 0, 2, 1, 4)
-        .reshape(calls, groups, local_rows, call_width)
-    )
+    by_clip_grad = grad_attended.reshape(clips_here, local_rows, width)
+    outgoing_grad = [
+        jnp.stack(
+            [
+                by_clip_grad[clip, :, at : at + call_width]
+                for clip in range(clips_here)
+                for at in range(call * call_width, width, part_width)
+            ]
+        )
+        for call in range(calls)
+    ]
     grad_parts = [
         exchange(outgoing_grad[call], "mp").reshape(seq_len, call_width) for call in range(calls)
     ]
 
-    def scatter_rows(grad, shape):
-        return lax.psum_scatter(
-            grad.astype(bf16).reshape(shape), "dp", scatter_dimension=1, tiled=True
-        )
-
-    grad_down = scatter_rows(dot(active, grad_final_low, TN), (ff // B, B, width))
-    grad_up = scatter_rows(dot(normed_two, grad_upper, TN), (row_blocks, B, ff))
-    grad_out = scatter_rows(dot(attended, grad_hidden_low, TN), (width // B, B, width))
+    grad_out = dot(attended, grad_hidden_low, TN).astype(bf16)
+    grad_up = dot(normed_two, grad_upper, TN).astype(bf16)
+    grad_parts[0], grad_out, grad_up = lax.optimization_barrier((grad_parts[0], grad_out, grad_up))
+
+    grad_down = scatter(grad_down.reshape(ff // B, B, width))
+    grad_up = scatter(grad_up.reshape(row_blocks, B, ff))
     early = jnp.concatenate(
         [
             jnp.sum(grad_hidden, axis=0),
             grad_gain_two,
             grad_shift_two,
             jnp.sum(grad_final, axis=0),
-            jnp.sum(grad_upper, axis=0, dtype=f32),
+            jnp.sum(
+                jnp.where(near_picks, jnp.sum(grad_upper, axis=0, dtype=f32).reshape(1, groups, -1), 0.0),
+                axis=1,
+            ).reshape(ff),
         ]
     )
-    early_total = sum_everywhere(early.reshape(-1, width))
-    by_group = jnp.concatenate(
-        [
-            grad_out.reshape(groups, -1, shard_rows, width),
-            grad_up.reshape(row_blocks, shard_rows, groups, group_ff).transpose(2, 0, 1, 3),
-            grad_down.reshape(groups, -1, shard_rows, width),
-        ],
-        axis=1,
-    )
-    own = jnp.sum(
-        exchange(by_group, "mp").reshape(groups, -1, shard_rows, width).astype(f32), axis=0
-    )
-    count = group_width // B
-    out_shard, up_shard, down_shard = own[:count], own[count : count + row_blocks], own[count + row_blocks :]
+    down_shard = sum_pieces(grad_down.reshape(groups, -1, shard_rows, width), "mp")
+    up_sent = grad_up.reshape(row_blocks, shard_rows, groups, group_ff).transpose(2, 0, 1, 3)
+    up_shard = sum_pieces(up_sent, "mp")
 
     pieces = []
     for call in range(calls):
@@ -451,49 +539,31 @@
             )
         )
     grad_proj = jnp.concatenate([piece[kind] for kind in range(3) for piece in pieces], axis=1)
+    grad_qkv = dot(normed_clip, grad_proj, TN).astype(bf16)
+    grad_proj, grad_qkv = lax.optimization_barrier((grad_proj, grad_qkv))
+    last_grads = jnp.concatenate(
+        [grad_qkv.reshape(row_blocks, B, 3 * part_width), grad_out.reshape(width // B, B, width)],
+        axis=2,
+    )
+    last_grads = scatter(last_grads)
+    grad_qkv, grad_out = last_grads[:, :, : 3 * part_width], last_grads[:, :, 3 * part_width :]
+    out_shard = sum_pieces(near_first(grad_out.reshape(groups, -1, shard_rows, width)), "mp")
     grad_normed_part = dot(grad_proj, qkv_weight, NT).astype(bf16)
-    grad_qkv = scatter_rows(
-        dot(normed_clip, grad_proj, TN), (row_blocks, B, 3 * part_width)
-    )
-    returned_grad = exchange(grad_normed_part.reshape(groups, local_rows, width), "mp")
-    grad_normed = jnp.sum(
-        returned_grad.reshape(clips_here, parts, local_rows, width).astype(f32), axis=1
-    ).reshape(tokens_here, width)
-    _, norm_one_pull = jax.vjp(layer_norm, tokens, norm_gains[0], shift_vectors[0])
-    tokens_part, grad_gain_one, grad_shift_one = norm_one_pull(grad_normed)
-    input_grad = (
-        (grad_hidden + tokens_part).reshape(clips_here, local_rows, width).transpose(1, 0, 2)
-    )
-    part_sums = jnp.sum(grad_proj, axis=0, dtype=f32).reshape(3, part_width)
-    placed_sums = jnp.where(
-        jnp.arange(parts)[:, None, None] == my_part, part_sums[None, ::2], 0.0
-    )
-    bias_rows = placed_sums.transpose(1, 0, 2).reshape(2, width)
-    late = jnp.concatenate([grad_gain_one[None], grad_shift_one[None], bias_rows])
-    late_total = sum_everywhere(late)
-    plain_total = jnp.concatenate([late_total[:2], early_total[:4]])
-    split_grad = jnp.concatenate(
-        [
-            late_total[2].reshape(groups, group_width),
-            late_total[3].reshape(groups, group_width),
-            early_total[4:].reshape(groups, group_ff),
-        ],
-        axis=1,
-    )
-    split_total = lax.dynamic_slice_in_dim(split_grad, group_index, 1, axis=0)
-
-    qkv_groups_grad = (
-        grad_qkv.reshape(row_blocks, shard_rows, 3, part_groups, group_width)
-        .transpose(3, 0, 1, 2, 4)
-        .reshape(1, part_groups, row_blocks, shard_rows, 3 * group_width)
-    )
-    here = jnp.arange(parts)[:, None, None, None, None] == my_part
-    qkv_sent = jnp.where(here, qkv_groups_grad, jnp.zeros((), bf16)).reshape(
-        groups, row_blocks, shard_rows, 3 * group_width
-    )
-    qkv_shard = jnp.sum(
-        exchange(qkv_sent, "mp").astype(f32), axis=0
-    ).reshape(row_blocks, shard_rows, 3, group_width)
+    pieces = near_first(grad_normed_part.reshape(groups, local_rows, width))
+    passed = send_steps(pieces, "mp")
+
+    first_group, second_group = [
+        grad_qkv.reshape(row_blocks, shard_rows, 3, part_groups, group_width)[:, :, :, at].reshape(
+            row_blocks, shard_rows, 3 * group_width
+        )
+        for at in range(part_groups)
+    ]
+    near_sent = jnp.where(low_half, second_group, first_group)
+    inner_sent = jnp.where(low_half, first_group, second_group)
+    near_got = lax.ppermute(near_sent, "mp", [(0, 1), (1, 3), (2, 0), (3, 2)])
+    inner_got = lax.ppermute(inner_sent, "mp", [(1, 2), (2, 1)])
+    qkv_shard = near_got.astype(f32) + jnp.where(outer, inner_sent, inner_got).astype(f32)
+    qkv_shard = qkv_shard.reshape(row_blocks, shard_rows, 3, group_width)
 
     grad_blocks = jnp.concatenate(
         [
@@ -522,9 +592,36 @@
         & (owners[None, None, :] == jnp.arange(shard_count)[None, :, None])
     ).astype(bf16)
     outgoing = jnp.einsum("cjk,krb->cjrb", select, grad_blocks, preferred_element_type=bf16)
+    sources = jnp.stack(passed).reshape(clips_here, parts, local_rows, width)
+    by_clip = jnp.sum(sources.astype(f32), axis=1)
+    grad_normed = jnp.where(my_clip == 0, by_clip, by_clip[::-1]).reshape(tokens_here, width)
+    _, norm_one_pull = jax.vjp(layer_norm, tokens, norm_gains[0], shift_vectors[0])
+    tokens_part, grad_gain_one, grad_shift_one = norm_one_pull(grad_normed)
+    input_grad = (
+        (grad_hidden + tokens_part).reshape(clips_here, local_rows, width).transpose(1, 0, 2)
+    )
+    part_sums = jnp.sum(grad_proj, axis=0, dtype=f32).reshape(3, part_width)
+    placed_sums = jnp.where(
+        jnp.arange(parts)[:, None, None] == my_part, part_sums[None, ::2], 0.0
+    )
+    bias_rows = placed_sums.transpose(1, 0, 2).reshape(2, width)
+    late = jnp.concatenate([grad_gain_one[None], grad_shift_one[None], bias_rows])
+    sums = sum_everywhere(jnp.concatenate([late, early.reshape(-1, width)]))
+    late_total, early_total = sums[:4], sums[4:]
+    plain_total = jnp.concatenate([late_total[:2], early_total[:4]])
+    split_grad = jnp.concatenate(
+        [
+            late_total[2].reshape(groups, group_width),
+            late_total[3].reshape(groups, group_width),
+            early_total[4:].reshape(groups, group_ff),
+        ],
+        axis=1,
+    )
+    split_total = lax.dynamic_slice_in_dim(split_grad, group_index, 1, axis=0)
+
+    incoming = lax.all_to_all(outgoing, "dp", split_axis=1, concat_axis=1, tiled=True)
     incoming = (
-        lax.all_to_all(outgoing, "dp", split_axis=1, concat_axis=1, tiled=True)
-        .astype(f32)
+        incoming.astype(f32)
         .reshape(cap_count, B, B)
     )
     slot_used = jnp.any(

time: 883 us -> 760 us (0.86)
  blocking collectives: 134 us -> 0 us
  matrix products: 170 us -> 111 us
  starting transfers between devices: 55.5 us -> 97.5 us
  waiting for transfers between devices: 273 us -> 305 us
  local copies, waits for them, and re-layouts: 77 us -> 48.5 us
  Pallas kernels: 101 us -> 119 us
    ppermute x10 -> x30, waiting for transfers between devices: 51.1 us -> 188 us  [the longest x9 103 us: send_all(): lax.ppermute(values, axis, [(i, i ^ step) for i in range(size)])]
    all_gather x3 -> x0, blocking collectives: 134 us -> none  [the longest x1 89.5 us: per_device(): split_all = lax.all_gather(split_vectors[0], 'mp', axis=0)]
    all_to_all x8 -> x5, waiting for transfers between devices: 94.6 us -> 22.1 us  [exchange(): return lax.all_to_all(values, axis, split_axis=0, concat_axis=0, tiled=True)]
    dot_general x12 -> x11, matrix products: 159 us -> 99.9 us  [dot(): return lax.dot_general(left, right, dims, preferred_element_type=f32)]
    ppermute x10 -> x30, starting transfers between devices: 10.7 us -> 69.6 us  [the longest x5 23.2 us: sum_everywhere(): other = lax.ppermute(values, axis, [(i, i ^ bit) for i in range(size)])]
    reduce_scatter x4 -> x3, waiting for transfers between devices: 96.2 us -> 71.4 us  [scatter(): return lax.psum_scatter(values, 'dp', scatter_dimension=1, tiled=True)]
    pallas_call x0 -> x1, Pallas kernels: none -> 16.7 us  [feed_up(): pl.pallas_call(partial(feed_kernel, tokens // 7), grid=(weight.shape[1] /...]
    all_to_all x8 -> x5, starting transfers between devices: 36 us -> 19.7 us  [exchange(): return lax.all_to_all(values, axis, split_axis=0, concat_axis=0, tiled=True)]
  transfers between devices with their start and end apart: 30 -> 44, of which waited for: 16 -> 23; matrix products, arithmetic and copies ran while one was open for 21% -> 14% of each run, Pallas kernels for 7% -> 11%
where the time goes in v2:
time: 760 us; the launch traced here: 752 us
  waiting for transfers between devices  305 us (40%)
  Pallas kernels  119 us (16%)
  matrix products  111 us (15%)
  starting transfers between devices  97.5 us (13%)
  other arithmetic  54.6 us (7%)
  local copies, waits for them, and re-layouts  48.5 us (6%)
  between operations  16.7 us (2%)
    ppermute x9, waiting for transfers between devices, send_all(): lax.ppermute(values, axis, [(i, i ^ step) for i in range(size)])  103 us
    dot_general x11, matrix products, dot(): return lax.dot_general(left, right, dims, preferred_element_type=f32)  99.9 us
    pallas_call x2, Pallas kernels, attend_backward(): pl.pallas_call(backward_kernel, grid=(pairs, tokens // row_block), in_spe...  71.9 us
    reduce_scatter x3, waiting for transfers between devices, scatter(): return lax.psum_scatter(values, 'dp', scatter_dimension=1, tiled=True)  71.4 us
    ppermute x12, waiting for transfers between devices, send_steps(): lax.ppermute(pieces[step], axis, [(i, i ^ step) for i in range(size)])  69.1 us
    pallas_call x2, Pallas kernels, attend_forward(): pl.pallas_call(partial(forward_kernel, chunk), grid=(pairs,), in_specs=[p...  30.1 us
    ppermute x5, starting transfers between devices, sum_everywhere(): other = lax.ppermute(values, axis, [(i, i ^ bit) for i in range(size)])  23.2 us
    all_to_all x5, waiting for transfers between devices, exchange(): return lax.all_to_all(values, axis, split_axis=0, concat_axis=0, tiled=True)  22.1 us
  transfers between devices with their start and end apart: 44, of which 23 were waited for; matrix products, arithmetic and copies ran while one was open for 14% of the time, Pallas kernels for 11%

profile of v2, /device:TPU:0, one launch (start us, length us, event | category | flops | bytes accessed | tf_op | source)
XLA Modules:
  0.0 752.3 jit_solution(17840743622046340600)
XLA Ops:
  29.1 10.2 %collective-permute-done.5 = bf16[1,10,16,1024]{3,2,1,0:T(8,128)(2,1)S(1)} collective-permute-done((bf16[1,10,16,1024]{3,2,1,0:T(8,128)(2,1)S(1)}, bf16[1,10,16,1024]{3,2,1,0:T(8,128)(2,1)S(1)}, u32[]{:S(2)}, u32[]{:S(2)}) %collective-permute-start.5) | collective-permute-done | bytes 327712 | tf_op jit(solution)/shard_map/ppermute | solution.py:332
  39.3 12.8 %collective-permute-done.6 = bf16[1,10,16,1024]{3,2,1,0:T(8,128)(2,1)S(1)} collective-permute-done((bf16[1,10,16,1024]{3,2,1,0:T(8,128)(2,1)S(1)}, bf16[1,10,16,1024]{3,2,1,0:T(8,128)(2,1)S(1)}, u32[]{:S(2)}, u32[]{:S(2)}) %collective-permute-start.6) | collective-permute-done | bytes 327712 | tf_op jit(solution)/shard_map/ppermute | solution.py:332
  70.4 9.1 %collective-permute-done.9 = bf16[8,16,1024]{2,1,0:T(8,128)(2,1)S(1)} collective-permute-done((bf16[8,16,1024]{2,1,0:T(8,128)(2,1)S(1)}, bf16[8,16,1024]{2,1,0:T(8,128)(2,1)S(1)}, u32[]{:S(2)}, u32[]{:S(2)}) %collective-permute-start.9) | collective-permute-done | bytes 262176 | tf_op jit(solution)/shard_map/ppermute | solution.py:332
  96.1 44.2 %collective-permute-done.2 = f32[1,1536]{1,0:T(1,128)S(1)} collective-permute-done((f32[1,1536]{1,0:T(1,128)S(1)}, f32[1,1536]{1,0:T(1,128)S(1)}, u32[]{:S(2)}, u32[]{:S(2)}) %collective-permute-start.2) | collective-permute-done | bytes 6176 | tf_op jit(solution)/shard_map/ppermute | solution.py:332
  140.3 20.4 %collective-permute-done.3 = f32[1,1536]{1,0:T(1,128)S(1)} collective-permute-done((f32[1,1536]{1,0:T(1,128)S(1)}, f32[1,1536]{1,0:T(1,128)S(1)}, u32[]{:S(2)}, u32[]{:S(2)}) %collective-permute-start.3) | collective-permute-done | bytes 6176 | tf_op jit(solution)/shard_map/ppermute | solution.py:332
  161.0 9.2 %add_convert_fusion.q_ref.k_ref.v_ref = bf16[1568,1536]{1,0:T(8,128)(2,1)} fusion(bf16[1568,1024]{1,0:T(8,128)(2,1)} %bitcast.5, bf16[1024,1536]{1,0:T(8,128)(2,1)} %bitcast.395, f32[1536]{0:T(1024)S(1)} %pad_maximum_fusion.15), kind=kOutput, calls=%fused_computation.4 | convolution fusion | flops 4937318400 | bytes 11180032 | tf_op jit(solution)/shard_map/dot_general | solution.py:35
  170.2 15.1 %shard_map.321 = (bf16[1568,256]{1,0:T(8,128)(2,1)}, f32[1568,256]{1,0:T(8,128)}) custom-call(s32[1]{0:T(128)} %dynamic_slice.47.valid_ref, bf16[1568,1536]{1,0:T(8,128)(2,1)} %add_convert_fusion.q_ref.k_ref.v_ref, bf16[1568,1536]{1,0:T(8,128)(2,1)} %add_convert_fusion.q_ref.k_ref.v_ref, bf16[1568,1536]{1,0:T(8,128)(2,1)} %add_convert_fusion.q_ref.k_ref.v_ref), custom_call_target="tpu_custom_call" | custom-call | flops 10070523904 | bytes 4816896 | tf_op jit(solution)/shard_map/pallas_call | solution.py:131
  189.0 15.0 %shard_map.322 = (bf16[1568,256]{1,0:T(8,128)(2,1)}, f32[1568,256]{1,0:T(8,128)}) custom-call(s32[1]{0:T(128)} %dynamic_slice.47.valid_ref, bf16[1568,1536]{1,0:T(8,128)(2,1)} %add_convert_fusion.q_ref.k_ref.v_ref, bf16[1568,1536]{1,0:T(8,128)(2,1)} %add_convert_fusion.q_ref.k_ref.v_ref, bf16[1568,1536]{1,0:T(8,128)(2,1)} %add_convert_fusion.q_ref.k_ref.v_ref), custom_call_target="tpu_custom_call" | custom-call | flops 10070523904 | bytes 4816896 | tf_op jit(solution)/shard_map/pallas_call | solution.py:131
  220.8 12.2 %all-to-all-done.2 = bf16[4,392,256]{2,1,0:T(8,128)(2,1)S(1)} async-done(((bf16[4,392,256]{2,1,0:T(8,128)(2,1)}), bf16[4,392,256]{2,1,0:T(8,128)(2,1)S(1)}, u32[]{:S(2)}, u32[]{:S(2)}) %all-to-all-start.2) | async-done | bytes 802848 | tf_op jit(solution)/shard_map/all_to_all | solution.py:309
  240.4 16.7 %shard_map.323 = (bf16[784,4096]{1,0:T(8,128)(2,1)}, bf16[784,4096]{1,0:T(8,128)(2,1)}) custom-call(bf16[784,1024]{1,0:T(8,128)(2,1)S(1)} %add_convert_fusion.1.normed_ref, bf16[1024,4096]{1,0:T(8,128)(2,1)} %bitcast.391, f32[1,4096]{1,0:T(1,128)S(1)} %bitcast.320), custom_call_target="tpu_custom_call" | custom-call | flops 6576668672 | bytes 21233664 | tf_op jit(solution)/shard_map/pallas_call | solution.py:287
  257.1 13.8 %fusion.86 = (f32[1024]{0:T(1024)S(1)}, f32[784,1024]{1,0:T(8,128)S(1)}, bf16[784,1024]{1,0:T(8,128)(2,1)}) fusion(f32[2,392,1024]{2,1,0:T(8,128)} %copy.288, pred[784]{0:T(1024)(128)(4,1)S(1)} %lt.87, f32[1024]{0:T(1024)S(1)} %bitcast.390, bf16[784,4096]{1,0:T(8,128)(2,1)} %get-tuple-element.40, bf16[4096,1024]{1,0:T(8,128)(2,1)} %bitcast.393, ...), kind=kOutput, calls=%fused_computation.242 | convolution fusion | flops 6582287360 | bytes 26063632 | tf_op jit(solution)/shard_map/dot_general | solution.py:35
  271.2 11.5 %convolution_convert_fusion.1 = bf16[4096,1024]{1,0:T(8,128)(2,1)} fusion(bf16[784,4096]{1,0:T(8,128)(2,1)S(1)} %copy-done.59, bf16[784,1024]{1,0:T(8,128)(2,1)S(1)} %convert_element_type.171), kind=kOutput, calls=%fused_computation.6 | convolution fusion | flops 6580862976 | bytes 16416768 | tf_op jit(solution)/shard_map/dot_general | solution.py:35
  282.7 13.2 %convert_reduce_fusion = (f32[4096]{0:T(1024)S(1)}, bf16[784,4096]{1,0:T(8,128)(2,1)}) fusion(bf16[784,4096]{1,0:T(8,128)(2,1)} %get-tuple-element.42, bf16[784,1024]{1,0:T(8,128)(2,1)S(1)} %convert_element_type.171, bf16[4096,1024]{1,0:T(8,128)(2,1)} %bitcast.394), kind=kOutput, calls=%fused_computation.1 | convolution fusion | flops 6592720896 | bytes 22855680 | tf_op jit(solution)/shard_map/dot_general | solution.py:35
  295.9 12.3 %multiply_reduce_fusion = (f32[1024]{0:T(1024)S(1)}, f32[784]{0:T(1024)S(1)}, f32[1024]{0:T(1024)S(1)}, f32[784,1024]{1,0:T(8,128)S(1)}) fusion(f32[784,1024]{1,0:T(8,128)S(1)} %copy-done.3, f32[784]{0:T(1024)S(1)} %fusion.75, f32[784]{0:T(1024)S(1)} %broadcast_multiply_fusion, f32[1024]{0:T(1024)S(1)} %bitcast.375, f32[1024]{0:T(1024)S(1)} %bitcast.379, ...), kind=kOutput, calls=%fused_computation.43 | convolution fusion | flops 6583890944 | bytes 21259456 | tf_op jit(solution)/shard_map/dot_general | solution.py:35
  323.5 14.0 %convolution_convert_fusion = bf16[1024,4096]{1,0:T(8,128)(2,1)} fusion(bf16[784,1024]{1,0:T(8,128)(2,1)S(1)} %add_convert_fusion.1.normed_ref, bf16[784,4096]{1,0:T(8,128)(2,1)} %get-tuple-element.331), kind=kOutput, calls=%fused_computation.5 | convolution fusion | flops 6580862976 | bytes 16416768 | tf_op jit(solution)/shard_map/dot_general | solution.py:35
  346.0 35.8 %shard_map.324 = (bf16[1568,256]{1,0:T(8,128)(2,1)}, bf16[1568,256]{1,0:T(8,128)(2,1)}, bf16[1568,256]{1,0:T(8,128)(2,1)}) custom-call(s32[1]{0:T(128)} %dynamic_slice.47.valid_ref, bf16[1568,1536]{1,0:T(8,128)(2,1)} %add_convert_fusion.q_ref.k_ref.v_ref, bf16[1568,1536]{1,0:T(8,128)(2,1)} %add_convert_fusion.q_ref.k_ref.v_ref, ...), custom_call_target="tpu_custom_call" | custom-call | flops 25176309760 | bytes 9633792 | tf_op jit(solution)/shard_map/pallas_call | solution.py:243
  384.8 36.1 %shard_map.325 = (bf16[1568,256]{1,0:T(8,128)(2,1)}, bf16[1568,256]{1,0:T(8,128)(2,1)}, bf16[1568,256]{1,0:T(8,128)(2,1)}) custom-call(s32[1]{0:T(128)} %dynamic_slice.47.valid_ref, bf16[1568,1536]{1,0:T(8,128)(2,1)} %add_convert_fusion.q_ref.k_ref.v_ref, bf16[1568,1536]{1,0:T(8,128)(2,1)} %add_convert_fusion.q_ref.k_ref.v_ref, ...), custom_call_target="tpu_custom_call" | custom-call | flops 25176309760 | bytes 9633792 | tf_op jit(solution)/shard_map/pallas_call | solution.py:243
  454.7 27.4 %collective-permute-done.11 = bf16[392,1024]{1,0:T(8,128)(2,1)S(1)} collective-permute-done((bf16[392,1024]{1,0:T(8,128)(2,1)}, bf16[392,1024]{1,0:T(8,128)(2,1)S(1)}, u32[]{:S(2)}, u32[]{:S(2)}) %collective-permute-start.11) | collective-permute-done | bytes 802848 | tf_op jit(solution)/shard_map/ppermute | solution.py:324
  482.1 23.2 %collective-permute-done.12 = bf16[392,1024]{1,0:T(8,128)(2,1)S(1)} collective-permute-done((bf16[392,1024]{1,0:T(8,128)(2,1)}, bf16[392,1024]{1,0:T(8,128)(2,1)S(1)}, u32[]{:S(2)}, u32[]{:S(2)}) %collective-permute-start.12) | collective-permute-done | bytes 802848 | tf_op jit(solution)/shard_map/ppermute | solution.py:324
  525.2 17.1 %collective-permute-start.28 = (f32[12,1024]{1,0:T(8,128)S(1)}, f32[12,1024]{1,0:T(8,128)S(1)}, u32[]{:S(2)}, u32[]{:S(2)}) collective-permute-start(f32[12,1024]{1,0:T(8,128)S(1)} %add.315), channel_id=1, source_target_pairs={{0,1},{1,0},{2,3},{3,2},{4,5},{5,4},{6,7},{7,6},{8,9},{9,8},{10,11... | collective-permute-start | bytes 147464 | tf_op jit(solution)/shard_map/ppermute | solution.py:348
  574.2 68.5 %reduce-scatter.6.cloned.1.call-done = bf16[8,16,4096]{2,1,0:T(8,128)(2,1)} async-done(((bf16[8,128,4096]{2,1,0:T(8,128)(2,1)}), bf16[8,16,4096]{2,1,0:T(8,128)(2,1)}) %reduce-scatter.6.cloned.1.call-update) | async-done | bytes 1048592 | tf_op jit(solution)/shard_map/reduce_scatter | solution.py:317
  658.8 10.6 %collective-permute-done.20 = bf16[8,16,1024]{2,1,0:T(8,128)(2,1)S(1)} collective-permute-done((bf16[8,16,1024]{2,1,0:T(8,128)(2,1)S(1)}, bf16[8,16,1024]{2,1,0:T(8,128)(2,1)S(1)}, u32[]{:S(2)}, u32[]{:S(2)}) %collective-permute-start.20) | collective-permute-done | bytes 262176 | tf_op jit(solution)/shard_map/ppermute | solution.py:324
  687.2 9.1 %all-to-all-done.5 = bf16[48,8,16,128]{3,2,0,1:T(8,128)(2,1)S(1)} async-done(((bf16[48,8,16,128]{3,2,0,1:T(8,128)(2,1)}), bf16[48,8,16,128]{3,2,0,1:T(8,128)(2,1)S(1)}, u32[]{:S(2)}, u32[]{:S(2)}) %all-to-all-start.5) | async-done | bytes 1572896 | tf_op jit(solution)/shard_map/all_to_all | solution.py:622
  725.7 12.7 %all-to-all-done.6 = bf16[48,8,16,128]{3,2,0,1:T(8,128)(2,1)} async-done(((bf16[48,8,16,128]{3,2,0,1:T(8,128)(2,1)}), bf16[48,8,16,128]{3,2,0,1:T(8,128)(2,1)}, u32[]{:S(2)}, u32[]{:S(2)}) %all-to-all-start.6) | async-done | bytes 1572896 | tf_op jit(solution)/shard_map/all_to_all | solution.py:638
  (385 shorter events, 265.3 us)
Async XLA Ops:
  7.2 153.8 %all-gather.5.cloned.1.call-start = ((), (), s32[]{:S(2)}) async-start(), calls=%async_computation.10 | async-start | bytes 3538944 | tf_op jit(solution)/shard_map/all_gather | solution.py:313
  21.8 212.8 %all-gather.7.cloned.1.call-start = ((), (), s32[]{:S(2)}) async-start(), calls=%async_computation.11 | async-start | bytes 2359296 | tf_op jit(solution)/shard_map/all_gather | solution.py:313
  26.6 25.5 %collective-permute-start.6 = (bf16[1,10,16,1024]{3,2,1,0:T(8,128)(2,1)S(1)}, bf16[1,10,16,1024]{3,2,1,0:T(8,128)(2,1)S(1)}, u32[]{:S(2)}, u32[]{:S(2)}) collective-permute-start(bf16[1,10,16,1024]{3,2,1,0:T(8,128)(2,1)S(1)} %maximum_bitcast_fusion.5), channel_id=1, source_target_pairs={{0,2},{1,3},{2,0},{3,1},{4,6},{5,7},{6,4},{7,5},{8,10},{9,11},{10,... | collective-permute-start | bytes 983048 | tf_op jit(solution)/shard_map/ppermute | solution.py:332
  27.7 24.4 %collective-permute-start.7 = (bf16[1,10,16,1024]{3,2,1,0:T(8,128)(2,1)S(1)}, bf16[1,10,16,1024]{3,2,1,0:T(8,128)(2,1)S(1)}, u32[]{:S(2)}, u32[]{:S(2)}) collective-permute-start(bf16[1,10,16,1024]{3,2,1,0:T(8,128)(2,1)S(1)} %maximum_bitcast_fusion.5), channel_id=1, source_target_pairs={{0,3},{1,2},{2,1},{3,0},{4,7},{5,6},{6,5},{7,4},{8,11},{9,10},{10,... | collective-permute-start | bytes 983048 | tf_op jit(solution)/shard_map/ppermute | solution.py:332
  53.0 187.4 %all-gather.9.cloned.1.call-start = ((), (), s32[]{:S(2)}) async-start(), calls=%async_computation.12 | async-start | bytes 9437184 | tf_op jit(solution)/shard_map/all_gather | solution.py:313
  54.3 202.8 %all-gather.11.cloned.1.call-start = ((), (), s32[]{:S(2)}) async-start(), calls=%async_computation.13 | async-start | bytes 9437184 | tf_op jit(solution)/shard_map/all_gather | solution.py:313
  85.9 75.1 %all-to-all-start = ((bf16[4,392,1024]{2,1,0:T(8,128)(2,1)}), bf16[4,392,1024]{2,1,0:T(8,128)(2,1)}, u32[]{:S(2)}, u32[]{:S(2)}) async-start(bf16[4,392,1024]{2,1,0:T(8,128)(2,1)} %bitcast.323), calls=%async_computation | async-start | bytes 6422528 | tf_op jit(solution)/shard_map/all_to_all | solution.py:309
  90.9 49.4 %collective-permute-start.2 = (f32[1,1536]{1,0:T(1,128)S(1)}, f32[1,1536]{1,0:T(1,128)S(1)}, u32[]{:S(2)}, u32[]{:S(2)}) collective-permute-start(f32[1,1536]{1,0:T(1,128)S(1)} %copy-done.44), channel_id=1, source_target_pairs={{0,1},{1,0},{2,3},{3,2},{4,5},{5,4},{6,7},{7,6},{8,9},{9,8},{10,11... | collective-permute-start | bytes 18440 | tf_op jit(solution)/shard_map/ppermute | solution.py:332
  93.0 67.8 %collective-permute-start.3 = (f32[1,1536]{1,0:T(1,128)S(1)}, f32[1,1536]{1,0:T(1,128)S(1)}, u32[]{:S(2)}, u32[]{:S(2)}) collective-permute-start(f32[1,1536]{1,0:T(1,128)S(1)} %copy-done.44), channel_id=1, source_target_pairs={{0,2},{1,3},{2,0},{3,1},{4,6},{5,7},{6,4},{7,5},{8,10},{9,11},{10,... | collective-permute-start | bytes 18440 | tf_op jit(solution)/shard_map/ppermute | solution.py:332
  95.3 65.4 %collective-permute-start.4 = (f32[1,1536]{1,0:T(1,128)S(1)}, f32[1,1536]{1,0:T(1,128)S(1)}, u32[]{:S(2)}, u32[]{:S(2)}) collective-permute-start(f32[1,1536]{1,0:T(1,128)S(1)} %copy-done.44), channel_id=1, source_target_pairs={{0,3},{1,2},{2,1},{3,0},{4,7},{5,6},{6,5},{7,4},{8,11},{9,10},{10,... | collective-permute-start | bytes 18440 | tf_op jit(solution)/shard_map/ppermute | solution.py:332
  209.0 23.9 %all-to-all-start.2 = ((bf16[4,392,256]{2,1,0:T(8,128)(2,1)}), bf16[4,392,256]{2,1,0:T(8,128)(2,1)S(1)}, u32[]{:S(2)}, u32[]{:S(2)}) async-start(bf16[4,392,256]{2,1,0:T(8,128)(2,1)} %bitcast.353), calls=%async_computation.2 | async-start | bytes 1605632 | tf_op jit(solution)/shard_map/all_to_all | solution.py:309
  342.4 41.5 %all-to-all-start.4 = ((bf16[4,392,256]{2,1,0:T(8,128)(2,1)}), bf16[4,392,256]{2,1,0:T(8,128)(2,1)S(1)}, u32[]{:S(2)}, u32[]{:S(2)}) async-start(bf16[4,392,256]{2,1,0:T(8,128)(2,1)} %pad_maximum_fusion.8), calls=%async_computation.4 | async-start | bytes 1605632 | tf_op jit(solution)/shard_map/all_to_all | solution.py:309
  345.9 201.6 %reduce-scatter.4.cloned.1.call-start = ((), (), s32[]{:S(2)}) async-start(), calls=%async_computation.14 | async-start | bytes 5898240 | tf_op jit(solution)/shard_map/reduce_scatter | solution.py:317
  434.5 133.3 %reduce-scatter.8.cloned.1.call-start = ((), (), s32[]{:S(2)}) async-start(), calls=%async_computation.16 | async-start | bytes 9437184 | tf_op jit(solution)/shard_map/reduce_scatter | solution.py:317
  435.1 207.6 %reduce-scatter.6.cloned.1.call-start = ((), (), s32[]{:S(2)}) async-start(), calls=%async_computation.15 | async-start | bytes 9437184 | tf_op jit(solution)/shard_map/reduce_scatter | solution.py:317
  447.1 35.0 %collective-permute-start.11 = (bf16[392,1024]{1,0:T(8,128)(2,1)}, bf16[392,1024]{1,0:T(8,128)(2,1)S(1)}, u32[]{:S(2)}, u32[]{:S(2)}) collective-permute-start(bf16[392,1024]{1,0:T(8,128)(2,1)} %get-tuple-element.267), channel_id=1, source_target_pairs={{0,1},{1,0},{2,3},{3,2},{4,5},{5,4},{6,7},{7,6},{8,9},{9,8},{10,11... | collective-permute-start | bytes 2408456 | tf_op jit(solution)/shard_map/ppermute | solution.py:324
  449.0 56.3 %collective-permute-start.12 = (bf16[392,1024]{1,0:T(8,128)(2,1)}, bf16[392,1024]{1,0:T(8,128)(2,1)S(1)}, u32[]{:S(2)}, u32[]{:S(2)}) collective-permute-start(bf16[392,1024]{1,0:T(8,128)(2,1)} %get-tuple-element.266), channel_id=1, source_target_pairs={{0,2},{1,3},{2,0},{3,1},{4,6},{5,7},{6,4},{7,5},{8,10},{9,11},{10,... | collective-permute-start | bytes 2408456 | tf_op jit(solution)/shard_map/ppermute | solution.py:324
  451.4 53.9 %collective-permute-start.13 = (bf16[392,1024]{1,0:T(8,128)(2,1)}, bf16[392,1024]{1,0:T(8,128)(2,1)S(1)}, u32[]{:S(2)}, u32[]{:S(2)}) collective-permute-start(bf16[392,1024]{1,0:T(8,128)(2,1)} %get-tuple-element.265), channel_id=1, source_target_pairs={{0,3},{1,2},{2,1},{3,0},{4,7},{5,6},{6,5},{7,4},{8,11},{9,10},{10,... | collective-permute-start | bytes 2408456 | tf_op jit(solution)/shard_map/ppermute | solution.py:324
  544.6 138.9 %collective-permute-start.29 = (f32[12,1024]{1,0:T(8,128)S(1)}, f32[12,1024]{1,0:T(8,128)}, u32[]{:S(2)}, u32[]{:S(2)}) collective-permute-start(f32[12,1024]{1,0:T(8,128)S(1)} %add.316), channel_id=1, source_target_pairs={{0,2},{1,3},{2,0},{3,1},{4,6},{5,7},{6,4},{7,5},{8,10},{9,11},{10,... | collective-permute-start | bytes 147464 | tf_op jit(solution)/shard_map/ppermute | solution.py:348
  569.8 78.2 %collective-permute-start.22 = (bf16[8,16,1024]{2,1,0:T(8,128)(2,1)}, bf16[8,16,1024]{2,1,0:T(8,128)(2,1)S(1)}, u32[]{:S(2)}, u32[]{:S(2)}) collective-permute-start(bf16[8,16,1024]{2,1,0:T(8,128)(2,1)} %get-tuple-element.285), channel_id=1, source_target_pairs={{0,1},{1,0},{2,3},{3,2},{4,5},{5,4},{6,7},{7,6},{8,9},{9,8},{10,11... | collective-permute-start | bytes 786440 | tf_op jit(solution)/shard_map/ppermute | solution.py:324
  571.3 79.2 %collective-permute-start.23 = (bf16[8,16,1024]{2,1,0:T(8,128)(2,1)}, bf16[8,16,1024]{2,1,0:T(8,128)(2,1)S(1)}, u32[]{:S(2)}, u32[]{:S(2)}) collective-permute-start(bf16[8,16,1024]{2,1,0:T(8,128)(2,1)} %get-tuple-element.287), channel_id=1, source_target_pairs={{0,2},{1,3},{2,0},{3,1},{4,6},{5,7},{6,4},{7,5},{8,10},{9,11},{10,... | collective-permute-start | bytes 786440 | tf_op jit(solution)/shard_map/ppermute | solution.py:324
  573.7 77.3 %collective-permute-start.24 = (bf16[8,16,1024]{2,1,0:T(8,128)(2,1)}, bf16[8,16,1024]{2,1,0:T(8,128)(2,1)S(1)}, u32[]{:S(2)}, u32[]{:S(2)}) collective-permute-start(bf16[8,16,1024]{2,1,0:T(8,128)(2,1)} %get-tuple-element.286), channel_id=1, source_target_pairs={{0,3},{1,2},{2,1},{3,0},{4,7},{5,6},{6,5},{7,4},{8,11},{9,10},{10,... | collective-permute-start | bytes 786440 | tf_op jit(solution)/shard_map/ppermute | solution.py:324
  671.8 24.5 %all-to-all-start.5 = ((bf16[48,8,16,128]{3,2,0,1:T(8,128)(2,1)}), bf16[48,8,16,128]{3,2,0,1:T(8,128)(2,1)S(1)}, u32[]{:S(2)}, u32[]{:S(2)}) async-start(bf16[48,8,16,128]{3,2,0,1:T(8,128)(2,1)} %copy.299), calls=%async_computation.8 | async-start | bytes 3145728 | tf_op jit(solution)/shard_map/all_to_all | solution.py:622
  713.0 25.3 %all-to-all-start.6 = ((bf16[48,8,16,128]{3,2,0,1:T(8,128)(2,1)}), bf16[48,8,16,128]{3,2,0,1:T(8,128)(2,1)}, u32[]{:S(2)}, u32[]{:S(2)}) async-start(bf16[48,8,16,128]{3,2,0,1:T(8,128)(2,1)} %copy.307), calls=%async_computation.9 | async-start | bytes 3145728 | tf_op jit(solution)/shard_map/all_to_all | solution.py:638
  (82 other events, 789.1 us)
Sparse Core Ops, SparseCore 0:
  21.9 35.4 all-gather.4
  59.9 27.8 all-gather.6
  90.3 54.2 all-gather.8
  146.3 54.2 all-gather.10
  434.7 57.7 reduce-scatter.3
  495.8 71.9 reduce-scatter.7
  571.3 71.3 reduce-scatter.5

commit v3 on v2

--- a/solution.py
+++ b/solution.py
@@ -146,9 +146,7 @@
             pltpu.VMEM((2, tokens, PAIR), bf16),
             pltpu.VMEM((2, tokens, tokens), f32),
         ],
-        compiler_params=pltpu.CompilerParams(
-            dimension_semantics=("arbitrary",), vmem_limit_bytes=58 * 2**20
-        ),
+        compiler_params=pltpu.CompilerParams(vmem_limit_bytes=58 * 2**20),
         cost_estimate=pl.CostEstimate(
             flops=16 * pairs * tokens * tokens * PAIR,
             bytes_accessed=pairs * tokens * PAIR * 12,
@@ -158,6 +156,7 @@
 
 
 def backward_kernel(
+    chunk,
     valid_ref,
     q_ref,
     k_ref,
@@ -172,96 +171,86 @@
     cot_ref,
     turned_ref,
 ):
-    step = pl.program_id(1)
-    rows = k_ref.shape[0]
-    lane = lane_index(q_ref.shape[0])
-
-    @pl.when(step == 0)
-    def _():
-        queries = q_ref[...].astype(f32) * scale_score
-        logs = log_ref[...]
-        log_high = logs.astype(bf16).astype(f32)
-        log_rest = logs - log_high
-        log_middle = log_rest.astype(bf16).astype(f32)
-        log_low = log_rest - log_middle
-        grad = grad_ref[...].astype(f32)
-        product = grad * out_ref[...].astype(f32)
-        product_high = product.astype(bf16)
-        product_low = (product - product_high.astype(f32)).astype(bf16)
-        source = lax.broadcasted_iota(jnp.int32, (PAIR, PAIR), 0)
-        target = lax.broadcasted_iota(jnp.int32, (PAIR, PAIR), 1)
-        place = jnp.where((source < HD) != (target < HD), -1.0, 0.0).astype(bf16)
-        delta = dot(product_high, place) + dot(product_low, place)
-        delta_high = delta.astype(bf16).astype(f32)
-        delta_low = delta - delta_high
+    tokens = q_ref.shape[0]
+    lane = lane_index(tokens)
+    queries = q_ref[...].astype(f32) * scale_score
+    logs = log_ref[...]
+    log_high = logs.astype(bf16).astype(f32)
+    log_rest = logs - log_high
+    log_middle = log_rest.astype(bf16).astype(f32)
+    log_low = log_rest - log_middle
+    grad = grad_ref[...].astype(f32)
+    product = grad * out_ref[...].astype(f32)
+    product_high = product.astype(bf16)
+    product_low = (product - product_high.astype(f32)).astype(bf16)
+    source = lax.broadcasted_iota(jnp.int32, (PAIR, PAIR), 0)
+    target = lax.broadcasted_iota(jnp.int32, (PAIR, PAIR), 1)
+    place = jnp.where((source < HD) != (target < HD), -1.0, 0.0).astype(bf16)
+    delta = dot(product_high, place) + dot(product_low, place)
+    delta_high = delta.astype(bf16).astype(f32)
+    delta_low = delta - delta_high
+    for head in range(2):
+        base = HD * (1 - head)
+        mine = own_lanes(lane, head)
+        mark = jnp.where(lane == base + 3, 1.0, 0.0)
+        other = jnp.where(lane == base + 2, log_low, mark)
+        other = jnp.where(lane == base + 1, log_middle, other)
+        other = jnp.where(lane == base, log_high, other)
+        query_ref[head] = jnp.where(mine, queries, other).astype(bf16)
+        other = jnp.where(lane == base + 1, delta_low, 0.0)
+        other = jnp.where(lane == base, delta_high, other)
+        cot_ref[head] = jnp.where(mine, grad, other).astype(bf16)
+
+    key_lane = lane_index(chunk)
+    for at in range(0, tokens, chunk):
+        rows = slice(at, at + chunk)
+        operands = key_operands(k_ref[rows], at, valid_ref[0])
+        wide_values = v_ref[rows].astype(f32)
+        turned_keys = jnp.transpose(k_ref[rows].astype(f32)).astype(bf16)
+        dk, dv = [], []
         for head in range(2):
             base = HD * (1 - head)
-            mine = own_lanes(lane, head)
-            mark = jnp.where(lane == base + 3, 1.0, 0.0)
-            other = jnp.where(lane == base + 2, log_low, mark)
-            other = jnp.where(lane == base + 1, log_middle, other)
-            other = jnp.where(lane == base, log_high, other)
-            query_ref[head] = jnp.where(mine, queries, other).astype(bf16)
-            other = jnp.where(lane == base + 1, delta_low, 0.0)
-            other = jnp.where(lane == base, delta_high, other)
-            cot_ref[head] = jnp.where(mine, grad, other).astype(bf16)
-        turned_ref[...] = jnp.zeros_like(turned_ref)
-
-    operands = key_operands(k_ref[...], step * rows, valid_ref[0])
-    key_lane = lane_index(rows)
-    wide_values = v_ref[...].astype(f32)
-    turned_keys = jnp.transpose(k_ref[...].astype(f32)).astype(bf16)
-    dk, dv = [], []
-    for head in range(2):
-        base = HD * (1 - head)
-        span = slice(HD * head, HD * head + HD)
-        pair_of_ones = jnp.where((key_lane == base) | (key_lane == base + 1), 1.0, 0.0)
-        values = jnp.where(own_lanes(key_lane, head), wide_values, pair_of_ones).astype(bf16)
-        weight = jnp.exp(dot(operands[head], query_ref[head], NT))
-        slope = (weight * dot(values, cot_ref[head], NT)).astype(bf16)
-        dv.append(dot(weight.astype(bf16), cot_ref[head]))
-        dk.append(dot(slope, query_ref[head]))
-        turned_ref[span] += dot(turned_keys[span], slope)
-    dk_ref[...] = jnp.where(key_lane < HD, dk[0], dk[1]).astype(bf16)
-    dv_ref[...] = jnp.where(key_lane < HD, dv[0], dv[1]).astype(bf16)
-
-    @pl.when(step == pl.num_programs(1) - 1)
-    def _():
-        dq_ref[...] = (jnp.transpose(turned_ref[...]) * scale_score).astype(bf16)
-
-
-def attend_backward(proj, grad, attended, logs, valid, first_pair, pairs, row_block):
+            span = slice(HD * head, HD * head + HD)
+            pair_of_ones = jnp.where((key_lane == base) | (key_lane == base + 1), 1.0, 0.0)
+            values = jnp.where(own_lanes(key_lane, head), wide_values, pair_of_ones).astype(bf16)
+            weight = jnp.exp(dot(operands[head], query_ref[head], NT))
+            slope = (weight * dot(values, cot_ref[head], NT)).astype(bf16)
+            dv.append(dot(weight.astype(bf16), cot_ref[head]))
+            dk.append(dot(slope, query_ref[head]))
+            term = dot(turned_keys[span], slope)
+            turned_ref[span] = term if at == 0 else turned_ref[span] + term
+        dk_ref[rows] = jnp.where(key_lane < HD, dk[0], dk[1]).astype(bf16)
+        dv_ref[rows] = jnp.where(key_lane < HD, dv[0], dv[1]).astype(bf16)
+    dq_ref[...] = (jnp.transpose(turned_ref[...]) * scale_score).astype(bf16)
+
+
+def attend_backward(proj, grad, attended, logs, valid, first_pair, pairs, chunk):
     tokens = proj.shape[0]
     per_part = proj.shape[1] // 3 // PAIR
 
-    def whole(at):
-        return pl.BlockSpec((tokens, PAIR), lambda pair, step: (0, at + pair))
-
-    def block(at):
-        return pl.BlockSpec((row_block, PAIR), lambda pair, step: (step, at + pair))
+    def pair_spec(at):
+        return pl.BlockSpec((tokens, PAIR), lambda pair: (0, at + pair))
 
     return pl.pallas_call(
-        backward_kernel,
-        grid=(pairs, tokens // row_block),
+        partial(backward_kernel, chunk),
+        grid=(pairs,),
         in_specs=[
             pl.BlockSpec(memory_space=pltpu.SMEM),
-            whole(first_pair),
-            block(per_part + first_pair),
-            block(2 * per_part + first_pair),
-            whole(0),
-            whole(0),
-            whole(0),
+            pair_spec(first_pair),
+            pair_spec(per_part + first_pair),
+            pair_spec(2 * per_part + first_pair),
+            pair_spec(0),
+            pair_spec(0),
+            pair_spec(0),
         ],
-        out_specs=[whole(0), block(0), block(0)],
+        out_specs=[pair_spec(0)] * 3,
         out_shape=[jax.ShapeDtypeStruct((tokens, pairs * PAIR), bf16)] * 3,
         scratch_shapes=[
             pltpu.VMEM((2, tokens, PAIR), bf16),
             pltpu.VMEM((2, tokens, PAIR), bf16),
             pltpu.VMEM((PAIR, tokens), f32),
         ],
-        compiler_params=pltpu.CompilerParams(
-            dimension_semantics=("arbitrary", "arbitrary"), vmem_limit_bytes=58 * 2**20
-        ),
+        compiler_params=pltpu.CompilerParams(vmem_limit_bytes=58 * 2**20),
         cost_estimate=pl.CostEstimate(
             flops=40 * pairs * tokens * tokens * PAIR,
             bytes_accessed=pairs * tokens * PAIR * 24,
@@ -294,9 +283,7 @@
         ],
         out_specs=[by_column, by_column],
         out_shape=[jax.ShapeDtypeStruct((tokens, weight.shape[1]), bf16)] * 2,
-        compiler_params=pltpu.CompilerParams(
-            dimension_semantics=("arbitrary",), vmem_limit_bytes=48 * 2**20
-        ),
+        compiler_params=pltpu.CompilerParams(vmem_limit_bytes=48 * 2**20),
         cost_estimate=pl.CostEstimate(
             flops=2 * tokens * width * weight.shape[1],
             bytes_accessed=4 * tokens * weight.shape[1] + 2 * width * weight.shape[1],

time: 760 us -> 752 us (0.989)
  Pallas kernels: 119 us -> 111 us
    pallas_call x2, Pallas kernels: 71.9 us -> 64 us  [attend_backward(): pl.pallas_call(partial(backward_kernel, chunk), grid=(pairs,), in_specs=[...]
where the time goes in v3:
time: 752 us; the launch traced here: 744 us
  waiting for transfers between devices  305 us (41%)
  matrix products  111 us (15%)
  Pallas kernels  111 us (15%)
  starting transfers between devices  97.2 us (13%)
  other arithmetic  54.4 us (7%)
  local copies, waits for them, and re-layouts  48.5 us (6%)
  between operations  16.5 us (2%)
    ppermute x9, waiting for transfers between devices, send_all(): lax.ppermute(values, axis, [(i, i ^ step) for i in range(size)])  103 us
    dot_general x11, matrix products, dot(): return lax.dot_general(left, right, dims, preferred_element_type=f32)  100 us
    reduce_scatter x3, waiting for transfers between devices, scatter(): return lax.psum_scatter(values, 'dp', scatter_dimension=1, tiled=True)  71.6 us
    ppermute x12, waiting for transfers between devices, send_steps(): lax.ppermute(pieces[step], axis, [(i, i ^ step) for i in range(size)])  68.9 us
    pallas_call x2, Pallas kernels, attend_backward(): pl.pallas_call(partial(backward_kernel, chunk), grid=(pairs,), in_specs=[...  64 us
    pallas_call x2, Pallas kernels, attend_forward(): pl.pallas_call(partial(forward_kernel, chunk), grid=(pairs,), in_specs=[p...  30.1 us
    ppermute x5, starting transfers between devices, sum_everywhere(): other = lax.ppermute(values, axis, [(i, i ^ bit) for i in range(size)])  23.1 us
    all_to_all x5, waiting for transfers between devices, exchange(): return lax.all_to_all(values, axis, split_axis=0, concat_axis=0, tiled=True)  22.1 us
  transfers between devices with their start and end apart: 44, of which 23 were waited for; matrix products, arithmetic and copies ran while one was open for 14% of the time, Pallas kernels for 11%

profile of v3, /device:TPU:0, one launch (start us, length us, event | category | flops | bytes accessed | tf_op | source)
XLA Modules:
  0.0 744.0 jit_solution(1977514368216036537)
XLA Ops:
  29.1 10.2 %collective-permute-done.5 = bf16[1,10,16,1024]{3,2,1,0:T(8,128)(2,1)S(1)} collective-permute-done((bf16[1,10,16,1024]{3,2,1,0:T(8,128)(2,1)S(1)}, bf16[1,10,16,1024]{3,2,1,0:T(8,128)(2,1)S(1)}, u32[]{:S(2)}, u32[]{:S(2)}) %collective-permute-start.5) | collective-permute-done | bytes 327712 | tf_op jit(solution)/shard_map/ppermute | solution.py:319
  39.3 12.8 %collective-permute-done.6 = bf16[1,10,16,1024]{3,2,1,0:T(8,128)(2,1)S(1)} collective-permute-done((bf16[1,10,16,1024]{3,2,1,0:T(8,128)(2,1)S(1)}, bf16[1,10,16,1024]{3,2,1,0:T(8,128)(2,1)S(1)}, u32[]{:S(2)}, u32[]{:S(2)}) %collective-permute-start.6) | collective-permute-done | bytes 327712 | tf_op jit(solution)/shard_map/ppermute | solution.py:319
  70.4 9.1 %collective-permute-done.9 = bf16[8,16,1024]{2,1,0:T(8,128)(2,1)S(1)} collective-permute-done((bf16[8,16,1024]{2,1,0:T(8,128)(2,1)S(1)}, bf16[8,16,1024]{2,1,0:T(8,128)(2,1)S(1)}, u32[]{:S(2)}, u32[]{:S(2)}) %collective-permute-start.9) | collective-permute-done | bytes 262176 | tf_op jit(solution)/shard_map/ppermute | solution.py:319
  96.0 44.2 %collective-permute-done.2 = f32[1,1536]{1,0:T(1,128)S(1)} collective-permute-done((f32[1,1536]{1,0:T(1,128)S(1)}, f32[1,1536]{1,0:T(1,128)S(1)}, u32[]{:S(2)}, u32[]{:S(2)}) %collective-permute-start.2) | collective-permute-done | bytes 6176 | tf_op jit(solution)/shard_map/ppermute | solution.py:319
  140.3 20.4 %collective-permute-done.3 = f32[1,1536]{1,0:T(1,128)S(1)} collective-permute-done((f32[1,1536]{1,0:T(1,128)S(1)}, f32[1,1536]{1,0:T(1,128)S(1)}, u32[]{:S(2)}, u32[]{:S(2)}) %collective-permute-start.3) | collective-permute-done | bytes 6176 | tf_op jit(solution)/shard_map/ppermute | solution.py:319
  161.0 9.2 %add_convert_fusion.q_ref.k_ref.v_ref = bf16[1568,1536]{1,0:T(8,128)(2,1)} fusion(bf16[1568,1024]{1,0:T(8,128)(2,1)} %bitcast.5, bf16[1024,1536]{1,0:T(8,128)(2,1)} %bitcast.395, f32[1536]{0:T(1024)S(1)} %pad_maximum_fusion.15), kind=kOutput, calls=%fused_computation.4 | convolution fusion | flops 4937318400 | bytes 11180032 | tf_op jit(solution)/shard_map/dot_general | solution.py:35
  170.2 15.1 %shard_map.321 = (bf16[1568,256]{1,0:T(8,128)(2,1)}, f32[1568,256]{1,0:T(8,128)}) custom-call(s32[1]{0:T(128)} %dynamic_slice.47.valid_ref, bf16[1568,1536]{1,0:T(8,128)(2,1)} %add_convert_fusion.q_ref.k_ref.v_ref, bf16[1568,1536]{1,0:T(8,128)(2,1)} %add_convert_fusion.q_ref.k_ref.v_ref, bf16[1568,1536]{1,0:T(8,128)(2,1)} %add_convert_fusion.q_ref.k_ref.v_ref), custom_call_target="tpu_custom_call" | custom-call | flops 10070523904 | bytes 4816896 | tf_op jit(solution)/shard_map/pallas_call | solution.py:131
  188.9 15.0 %shard_map.322 = (bf16[1568,256]{1,0:T(8,128)(2,1)}, f32[1568,256]{1,0:T(8,128)}) custom-call(s32[1]{0:T(128)} %dynamic_slice.47.valid_ref, bf16[1568,1536]{1,0:T(8,128)(2,1)} %add_convert_fusion.q_ref.k_ref.v_ref, bf16[1568,1536]{1,0:T(8,128)(2,1)} %add_convert_fusion.q_ref.k_ref.v_ref, bf16[1568,1536]{1,0:T(8,128)(2,1)} %add_convert_fusion.q_ref.k_ref.v_ref), custom_call_target="tpu_custom_call" | custom-call | flops 10070523904 | bytes 4816896 | tf_op jit(solution)/shard_map/pallas_call | solution.py:131
  220.5 12.2 %all-to-all-done.2 = bf16[4,392,256]{2,1,0:T(8,128)(2,1)S(1)} async-done(((bf16[4,392,256]{2,1,0:T(8,128)(2,1)}), bf16[4,392,256]{2,1,0:T(8,128)(2,1)S(1)}, u32[]{:S(2)}, u32[]{:S(2)}) %all-to-all-start.2) | async-done | bytes 802848 | tf_op jit(solution)/shard_map/all_to_all | solution.py:296
  240.1 16.7 %shard_map.323 = (bf16[784,4096]{1,0:T(8,128)(2,1)}, bf16[784,4096]{1,0:T(8,128)(2,1)}) custom-call(bf16[784,1024]{1,0:T(8,128)(2,1)S(1)} %add_convert_fusion.1.normed_ref, bf16[1024,4096]{1,0:T(8,128)(2,1)} %bitcast.391, f32[1,4096]{1,0:T(1,128)S(1)} %bitcast.320), custom_call_target="tpu_custom_call" | custom-call | flops 6576668672 | bytes 21233664 | tf_op jit(solution)/shard_map/pallas_call | solution.py:276
  256.8 13.8 %fusion.86 = (f32[1024]{0:T(1024)S(1)}, f32[784,1024]{1,0:T(8,128)S(1)}, bf16[784,1024]{1,0:T(8,128)(2,1)}) fusion(f32[2,392,1024]{2,1,0:T(8,128)} %copy.288, pred[784]{0:T(1024)(128)(4,1)S(1)} %lt.87, f32[1024]{0:T(1024)S(1)} %bitcast.390, bf16[784,4096]{1,0:T(8,128)(2,1)} %get-tuple-element.40, bf16[4096,1024]{1,0:T(8,128)(2,1)} %bitcast.393, ...), kind=kOutput, calls=%fused_computation.242 | convolution fusion | flops 6582287360 | bytes 26063632 | tf_op jit(solution)/shard_map/dot_general | solution.py:35
  270.9 11.8 %convolution_convert_fusion.1 = bf16[4096,1024]{1,0:T(8,128)(2,1)} fusion(bf16[784,4096]{1,0:T(8,128)(2,1)S(1)} %copy-done.59, bf16[784,1024]{1,0:T(8,128)(2,1)S(1)} %convert_element_type.171), kind=kOutput, calls=%fused_computation.6 | convolution fusion | flops 6580862976 | bytes 16416768 | tf_op jit(solution)/shard_map/dot_general | solution.py:35
  282.7 13.2 %convert_reduce_fusion = (f32[4096]{0:T(1024)S(1)}, bf16[784,4096]{1,0:T(8,128)(2,1)}) fusion(bf16[784,4096]{1,0:T(8,128)(2,1)} %get-tuple-element.42, bf16[784,1024]{1,0:T(8,128)(2,1)S(1)} %convert_element_type.171, bf16[4096,1024]{1,0:T(8,128)(2,1)} %bitcast.394), kind=kOutput, calls=%fused_computation.1 | convolution fusion | flops 6592720896 | bytes 22855680 | tf_op jit(solution)/shard_map/dot_general | solution.py:35
  295.9 12.3 %multiply_reduce_fusion = (f32[1024]{0:T(1024)S(1)}, f32[784]{0:T(1024)S(1)}, f32[1024]{0:T(1024)S(1)}, f32[784,1024]{1,0:T(8,128)S(1)}) fusion(f32[784,1024]{1,0:T(8,128)S(1)} %copy-done.3, f32[784]{0:T(1024)S(1)} %fusion.75, f32[784]{0:T(1024)S(1)} %broadcast_multiply_fusion, f32[1024]{0:T(1024)S(1)} %bitcast.375, f32[1024]{0:T(1024)S(1)} %bitcast.379, ...), kind=kOutput, calls=%fused_computation.43 | convolution fusion | flops 6583890944 | bytes 21259456 | tf_op jit(solution)/shard_map/dot_general | solution.py:35
  323.4 14.0 %convolution_convert_fusion = bf16[1024,4096]{1,0:T(8,128)(2,1)} fusion(bf16[784,1024]{1,0:T(8,128)(2,1)S(1)} %add_convert_fusion.1.normed_ref, bf16[784,4096]{1,0:T(8,128)(2,1)} %get-tuple-element.331), kind=kOutput, calls=%fused_computation.5 | convolution fusion | flops 6580862976 | bytes 16416768 | tf_op jit(solution)/shard_map/dot_general | solution.py:35
  346.0 31.6 %shard_map.324 = (bf16[1568,256]{1,0:T(8,128)(2,1)}, bf16[1568,256]{1,0:T(8,128)(2,1)}, bf16[1568,256]{1,0:T(8,128)(2,1)}) custom-call(s32[1]{0:T(128)} %dynamic_slice.47.valid_ref, bf16[1568,1536]{1,0:T(8,128)(2,1)} %add_convert_fusion.q_ref.k_ref.v_ref, bf16[1568,1536]{1,0:T(8,128)(2,1)} %add_convert_fusion.q_ref.k_ref.v_ref, ...), custom_call_target="tpu_custom_call" | custom-call | flops 25176309760 | bytes 9633792 | tf_op jit(solution)/shard_map/pallas_call | solution.py:234
  380.6 32.4 %shard_map.325 = (bf16[1568,256]{1,0:T(8,128)(2,1)}, bf16[1568,256]{1,0:T(8,128)(2,1)}, bf16[1568,256]{1,0:T(8,128)(2,1)}) custom-call(s32[1]{0:T(128)} %dynamic_slice.47.valid_ref, bf16[1568,1536]{1,0:T(8,128)(2,1)} %add_convert_fusion.q_ref.k_ref.v_ref, bf16[1568,1536]{1,0:T(8,128)(2,1)} %add_convert_fusion.q_ref.k_ref.v_ref, ...), custom_call_target="tpu_custom_call" | custom-call | flops 25176309760 | bytes 9633792 | tf_op jit(solution)/shard_map/pallas_call | solution.py:234
  446.6 27.5 %collective-permute-done.11 = bf16[392,1024]{1,0:T(8,128)(2,1)S(1)} collective-permute-done((bf16[392,1024]{1,0:T(8,128)(2,1)}, bf16[392,1024]{1,0:T(8,128)(2,1)S(1)}, u32[]{:S(2)}, u32[]{:S(2)}) %collective-permute-start.11) | collective-permute-done | bytes 802848 | tf_op jit(solution)/shard_map/ppermute | solution.py:311
  474.0 23.2 %collective-permute-done.12 = bf16[392,1024]{1,0:T(8,128)(2,1)S(1)} collective-permute-done((bf16[392,1024]{1,0:T(8,128)(2,1)}, bf16[392,1024]{1,0:T(8,128)(2,1)S(1)}, u32[]{:S(2)}, u32[]{:S(2)}) %collective-permute-start.12) | collective-permute-done | bytes 802848 | tf_op jit(solution)/shard_map/ppermute | solution.py:311
  517.1 16.9 %collective-permute-start.28 = (f32[12,1024]{1,0:T(8,128)S(1)}, f32[12,1024]{1,0:T(8,128)S(1)}, u32[]{:S(2)}, u32[]{:S(2)}) collective-permute-start(f32[12,1024]{1,0:T(8,128)S(1)} %add.315), channel_id=1, source_target_pairs={{0,1},{1,0},{2,3},{3,2},{4,5},{5,4},{6,7},{7,6},{8,9},{9,8},{10,11... | collective-permute-start | bytes 147464 | tf_op jit(solution)/shard_map/ppermute | solution.py:335
  566.2 68.5 %reduce-scatter.6.cloned.1.call-done = bf16[8,16,4096]{2,1,0:T(8,128)(2,1)} async-done(((bf16[8,128,4096]{2,1,0:T(8,128)(2,1)}), bf16[8,16,4096]{2,1,0:T(8,128)(2,1)}) %reduce-scatter.6.cloned.1.call-update) | async-done | bytes 1048592 | tf_op jit(solution)/shard_map/reduce_scatter | solution.py:304
  650.8 10.6 %collective-permute-done.20 = bf16[8,16,1024]{2,1,0:T(8,128)(2,1)S(1)} collective-permute-done((bf16[8,16,1024]{2,1,0:T(8,128)(2,1)S(1)}, bf16[8,16,1024]{2,1,0:T(8,128)(2,1)S(1)}, u32[]{:S(2)}, u32[]{:S(2)}) %collective-permute-start.20) | collective-permute-done | bytes 262176 | tf_op jit(solution)/shard_map/ppermute | solution.py:311
  678.9 9.4 %all-to-all-done.5 = bf16[48,8,16,128]{3,2,0,1:T(8,128)(2,1)S(1)} async-done(((bf16[48,8,16,128]{3,2,0,1:T(8,128)(2,1)}), bf16[48,8,16,128]{3,2,0,1:T(8,128)(2,1)S(1)}, u32[]{:S(2)}, u32[]{:S(2)}) %all-to-all-start.5) | async-done | bytes 1572896 | tf_op jit(solution)/shard_map/all_to_all | solution.py:609
  717.6 12.7 %all-to-all-done.6 = bf16[48,8,16,128]{3,2,0,1:T(8,128)(2,1)} async-done(((bf16[48,8,16,128]{3,2,0,1:T(8,128)(2,1)}), bf16[48,8,16,128]{3,2,0,1:T(8,128)(2,1)}, u32[]{:S(2)}, u32[]{:S(2)}) %all-to-all-start.6) | async-done | bytes 1572896 | tf_op jit(solution)/shard_map/all_to_all | solution.py:625
  (385 shorter events, 264.9 us)
Async XLA Ops:
  7.2 153.8 %all-gather.5.cloned.1.call-start = ((), (), s32[]{:S(2)}) async-start(), calls=%async_computation.10 | async-start | bytes 3538944 | tf_op jit(solution)/shard_map/all_gather | solution.py:300
  21.8 212.5 %all-gather.7.cloned.1.call-start = ((), (), s32[]{:S(2)}) async-start(), calls=%async_computation.11 | async-start | bytes 2359296 | tf_op jit(solution)/shard_map/all_gather | solution.py:300
  26.6 25.5 %collective-permute-start.6 = (bf16[1,10,16,1024]{3,2,1,0:T(8,128)(2,1)S(1)}, bf16[1,10,16,1024]{3,2,1,0:T(8,128)(2,1)S(1)}, u32[]{:S(2)}, u32[]{:S(2)}) collective-permute-start(bf16[1,10,16,1024]{3,2,1,0:T(8,128)(2,1)S(1)} %maximum_bitcast_fusion.5), channel_id=1, source_target_pairs={{0,2},{1,3},{2,0},{3,1},{4,6},{5,7},{6,4},{7,5},{8,10},{9,11},{10,... | collective-permute-start | bytes 983048 | tf_op jit(solution)/shard_map/ppermute | solution.py:319
  27.7 24.4 %collective-permute-start.7 = (bf16[1,10,16,1024]{3,2,1,0:T(8,128)(2,1)S(1)}, bf16[1,10,16,1024]{3,2,1,0:T(8,128)(2,1)S(1)}, u32[]{:S(2)}, u32[]{:S(2)}) collective-permute-start(bf16[1,10,16,1024]{3,2,1,0:T(8,128)(2,1)S(1)} %maximum_bitcast_fusion.5), channel_id=1, source_target_pairs={{0,3},{1,2},{2,1},{3,0},{4,7},{5,6},{6,5},{7,4},{8,11},{9,10},{10,... | collective-permute-start | bytes 983048 | tf_op jit(solution)/shard_map/ppermute | solution.py:319
  53.0 187.1 %all-gather.9.cloned.1.call-start = ((), (), s32[]{:S(2)}) async-start(), calls=%async_computation.12 | async-start | bytes 9437184 | tf_op jit(solution)/shard_map/all_gather | solution.py:300
  54.3 202.5 %all-gather.11.cloned.1.call-start = ((), (), s32[]{:S(2)}) async-start(), calls=%async_computation.13 | async-start | bytes 9437184 | tf_op jit(solution)/shard_map/all_gather | solution.py:300
  85.9 75.0 %all-to-all-start = ((bf16[4,392,1024]{2,1,0:T(8,128)(2,1)}), bf16[4,392,1024]{2,1,0:T(8,128)(2,1)}, u32[]{:S(2)}, u32[]{:S(2)}) async-start(bf16[4,392,1024]{2,1,0:T(8,128)(2,1)} %bitcast.323), calls=%async_computation | async-start | bytes 6422528 | tf_op jit(solution)/shard_map/all_to_all | solution.py:296
  90.9 49.4 %collective-permute-start.2 = (f32[1,1536]{1,0:T(1,128)S(1)}, f32[1,1536]{1,0:T(1,128)S(1)}, u32[]{:S(2)}, u32[]{:S(2)}) collective-permute-start(f32[1,1536]{1,0:T(1,128)S(1)} %copy-done.44), channel_id=1, source_target_pairs={{0,1},{1,0},{2,3},{3,2},{4,5},{5,4},{6,7},{7,6},{8,9},{9,8},{10,11... | collective-permute-start | bytes 18440 | tf_op jit(solution)/shard_map/ppermute | solution.py:319
  92.9 67.8 %collective-permute-start.3 = (f32[1,1536]{1,0:T(1,128)S(1)}, f32[1,1536]{1,0:T(1,128)S(1)}, u32[]{:S(2)}, u32[]{:S(2)}) collective-permute-start(f32[1,1536]{1,0:T(1,128)S(1)} %copy-done.44), channel_id=1, source_target_pairs={{0,2},{1,3},{2,0},{3,1},{4,6},{5,7},{6,4},{7,5},{8,10},{9,11},{10,... | collective-permute-start | bytes 18440 | tf_op jit(solution)/shard_map/ppermute | solution.py:319
  95.3 65.4 %collective-permute-start.4 = (f32[1,1536]{1,0:T(1,128)S(1)}, f32[1,1536]{1,0:T(1,128)S(1)}, u32[]{:S(2)}, u32[]{:S(2)}) collective-permute-start(f32[1,1536]{1,0:T(1,128)S(1)} %copy-done.44), channel_id=1, source_target_pairs={{0,3},{1,2},{2,1},{3,0},{4,7},{5,6},{6,5},{7,4},{8,11},{9,10},{10,... | collective-permute-start | bytes 18440 | tf_op jit(solution)/shard_map/ppermute | solution.py:319
  208.9 23.7 %all-to-all-start.2 = ((bf16[4,392,256]{2,1,0:T(8,128)(2,1)}), bf16[4,392,256]{2,1,0:T(8,128)(2,1)S(1)}, u32[]{:S(2)}, u32[]{:S(2)}) async-start(bf16[4,392,256]{2,1,0:T(8,128)(2,1)} %bitcast.353), calls=%async_computation.2 | async-start | bytes 1605632 | tf_op jit(solution)/shard_map/all_to_all | solution.py:296
  342.4 37.3 %all-to-all-start.4 = ((bf16[4,392,256]{2,1,0:T(8,128)(2,1)}), bf16[4,392,256]{2,1,0:T(8,128)(2,1)S(1)}, u32[]{:S(2)}, u32[]{:S(2)}) async-start(bf16[4,392,256]{2,1,0:T(8,128)(2,1)} %pad_maximum_fusion.8), calls=%async_computation.4 | async-start | bytes 1605632 | tf_op jit(solution)/shard_map/all_to_all | solution.py:296
  345.9 193.4 %reduce-scatter.4.cloned.1.call-start = ((), (), s32[]{:S(2)}) async-start(), calls=%async_computation.14 | async-start | bytes 5898240 | tf_op jit(solution)/shard_map/reduce_scatter | solution.py:304
  426.6 133.2 %reduce-scatter.8.cloned.1.call-start = ((), (), s32[]{:S(2)}) async-start(), calls=%async_computation.16 | async-start | bytes 9437184 | tf_op jit(solution)/shard_map/reduce_scatter | solution.py:304
  427.2 207.5 %reduce-scatter.6.cloned.1.call-start = ((), (), s32[]{:S(2)}) async-start(), calls=%async_computation.15 | async-start | bytes 9437184 | tf_op jit(solution)/shard_map/reduce_scatter | solution.py:304
  439.0 35.0 %collective-permute-start.11 = (bf16[392,1024]{1,0:T(8,128)(2,1)}, bf16[392,1024]{1,0:T(8,128)(2,1)S(1)}, u32[]{:S(2)}, u32[]{:S(2)}) collective-permute-start(bf16[392,1024]{1,0:T(8,128)(2,1)} %get-tuple-element.267), channel_id=1, source_target_pairs={{0,1},{1,0},{2,3},{3,2},{4,5},{5,4},{6,7},{7,6},{8,9},{9,8},{10,11... | collective-permute-start | bytes 2408456 | tf_op jit(solution)/shard_map/ppermute | solution.py:311
  440.9 56.3 %collective-permute-start.12 = (bf16[392,1024]{1,0:T(8,128)(2,1)}, bf16[392,1024]{1,0:T(8,128)(2,1)S(1)}, u32[]{:S(2)}, u32[]{:S(2)}) collective-permute-start(bf16[392,1024]{1,0:T(8,128)(2,1)} %get-tuple-element.266), channel_id=1, source_target_pairs={{0,2},{1,3},{2,0},{3,1},{4,6},{5,7},{6,4},{7,5},{8,10},{9,11},{10,... | collective-permute-start | bytes 2408456 | tf_op jit(solution)/shard_map/ppermute | solution.py:311
  443.3 53.9 %collective-permute-start.13 = (bf16[392,1024]{1,0:T(8,128)(2,1)}, bf16[392,1024]{1,0:T(8,128)(2,1)S(1)}, u32[]{:S(2)}, u32[]{:S(2)}) collective-permute-start(bf16[392,1024]{1,0:T(8,128)(2,1)} %get-tuple-element.265), channel_id=1, source_target_pairs={{0,3},{1,2},{2,1},{3,0},{4,7},{5,6},{6,5},{7,4},{8,11},{9,10},{10,... | collective-permute-start | bytes 2408456 | tf_op jit(solution)/shard_map/ppermute | solution.py:311
  536.3 138.9 %collective-permute-start.29 = (f32[12,1024]{1,0:T(8,128)S(1)}, f32[12,1024]{1,0:T(8,128)}, u32[]{:S(2)}, u32[]{:S(2)}) collective-permute-start(f32[12,1024]{1,0:T(8,128)S(1)} %add.316), channel_id=1, source_target_pairs={{0,2},{1,3},{2,0},{3,1},{4,6},{5,7},{6,4},{7,5},{8,10},{9,11},{10,... | collective-permute-start | bytes 147464 | tf_op jit(solution)/shard_map/ppermute | solution.py:335
  561.8 78.2 %collective-permute-start.22 = (bf16[8,16,1024]{2,1,0:T(8,128)(2,1)}, bf16[8,16,1024]{2,1,0:T(8,128)(2,1)S(1)}, u32[]{:S(2)}, u32[]{:S(2)}) collective-permute-start(bf16[8,16,1024]{2,1,0:T(8,128)(2,1)} %get-tuple-element.285), channel_id=1, source_target_pairs={{0,1},{1,0},{2,3},{3,2},{4,5},{5,4},{6,7},{7,6},{8,9},{9,8},{10,11... | collective-permute-start | bytes 786440 | tf_op jit(solution)/shard_map/ppermute | solution.py:311
  563.3 79.2 %collective-permute-start.23 = (bf16[8,16,1024]{2,1,0:T(8,128)(2,1)}, bf16[8,16,1024]{2,1,0:T(8,128)(2,1)S(1)}, u32[]{:S(2)}, u32[]{:S(2)}) collective-permute-start(bf16[8,16,1024]{2,1,0:T(8,128)(2,1)} %get-tuple-element.287), channel_id=1, source_target_pairs={{0,2},{1,3},{2,0},{3,1},{4,6},{5,7},{6,4},{7,5},{8,10},{9,11},{10,... | collective-permute-start | bytes 786440 | tf_op jit(solution)/shard_map/ppermute | solution.py:311
  565.7 77.3 %collective-permute-start.24 = (bf16[8,16,1024]{2,1,0:T(8,128)(2,1)}, bf16[8,16,1024]{2,1,0:T(8,128)(2,1)S(1)}, u32[]{:S(2)}, u32[]{:S(2)}) collective-permute-start(bf16[8,16,1024]{2,1,0:T(8,128)(2,1)} %get-tuple-element.286), channel_id=1, source_target_pairs={{0,3},{1,2},{2,1},{3,0},{4,7},{5,6},{6,5},{7,4},{8,11},{9,10},{10,... | collective-permute-start | bytes 786440 | tf_op jit(solution)/shard_map/ppermute | solution.py:311
  663.7 24.5 %all-to-all-start.5 = ((bf16[48,8,16,128]{3,2,0,1:T(8,128)(2,1)}), bf16[48,8,16,128]{3,2,0,1:T(8,128)(2,1)S(1)}, u32[]{:S(2)}, u32[]{:S(2)}) async-start(bf16[48,8,16,128]{3,2,0,1:T(8,128)(2,1)} %copy.299), calls=%async_computation.8 | async-start | bytes 3145728 | tf_op jit(solution)/shard_map/all_to_all | solution.py:609
  704.9 25.3 %all-to-all-start.6 = ((bf16[48,8,16,128]{3,2,0,1:T(8,128)(2,1)}), bf16[48,8,16,128]{3,2,0,1:T(8,128)(2,1)}, u32[]{:S(2)}, u32[]{:S(2)}) async-start(bf16[48,8,16,128]{3,2,0,1:T(8,128)(2,1)} %copy.307), calls=%async_computation.9 | async-start | bytes 3145728 | tf_op jit(solution)/shard_map/all_to_all | solution.py:625
  (82 other events, 781.8 us)
Sparse Core Ops, SparseCore 0:
  21.9 35.4 all-gather.4
  59.9 27.8 all-gather.6
  90.3 54.2 all-gather.8
  146.3 54.2 all-gather.10
  426.7 57.7 reduce-scatter.3
  487.9 71.8 reduce-scatter.7
  563.2 71.3 reduce-scatter.5
